TPU v7x, 32 devices: a whole 2x2x4 slice. The times are simulated.
32 devices in a mesh: pipe: 4 (over z), expert: 4 (over y, x), tensor: 2 (over core).
Axes of the slice: x: 2, y: 2, z: 4, core: 2. Of those that a mesh axis runs over, the one named last changes fastest.
Arguments:
- inputs_prev: bfloat16 [4, 512, 3584], P('pipe', 'expert', 'tensor'), may hold values from -6 to 6
- cotangent_next: bfloat16 [4, 512, 3584], P('pipe', 'expert', 'tensor'), may hold values from -6 to 6
- saved_input: bfloat16 [4, 512, 3584], P('pipe', 'expert', 'tensor'), may hold values from -6 to 6
- expert_ids: int32 [2, 4, 512, 8], P(None, 'pipe', 'expert'), may hold values from 0 to 255, as said below
- keep_mask: int32 [2, 4, 512, 8], P(None, 'pipe', 'expert'), may hold values from 0 to 1, as said below
- slot_pos: int32 [2, 4, 512, 8], P(None, 'pipe', 'expert'), may hold values from 0 to 3, as said below
- weight_q: int32 [2, 4, 512, 8], P(None, 'pipe', 'expert'), may hold values from 1 to 4095
- gate_routed: bfloat16 [4, 4, 3584, 512], P('pipe', 'expert', None, 'tensor'), may hold values from -0.09375 to 0.09375
- up_routed: bfloat16 [4, 4, 3584, 512], P('pipe', 'expert', None, 'tensor'), may hold values from -0.09375 to 0.09375
- down_routed: bfloat16 [4, 4, 512, 3584], P('pipe', 'expert', 'tensor'), may hold values from -0.1875 to 0.1875
- gate_shared: bfloat16 [4, 3584, 1024], P('pipe', None, 'tensor'), may hold values from -0.09375 to 0.09375
- up_shared: bfloat16 [4, 3584, 1024], P('pipe', None, 'tensor'), may hold values from -0.09375 to 0.09375
- down_shared: bfloat16 [4, 1024, 3584], P('pipe', 'tensor'), may hold values from -0.1875 to 0.1875
Outputs:
- out_act: bfloat16 [4, 512, 3584], P('pipe', 'expert', 'tensor')
- in_grad: bfloat16 [4, 512, 3584], P('pipe', 'expert', 'tensor')
Inputs may be any that keep to these rules, and one draw needn't show every extreme that they name: `expert_ids`: each row names 8 different experts; in every section and micro-batch one expert below 2 is named by every row. `keep_mask`: 1 only where the expert named is below 2; in one block of 128 rows no expert has more than 4 kept choices, and in every section and micro-batch one expert has exactly 4 in every block. `slot_pos`: kept choices of one block naming the same expert hold different slots; 0 where keep_mask is 0.
All inputs are finite; a program needn't handle non-finite values.
Results may differ from a plain program's by a relative error of at most 0.005.
Values may be sent and summed in bfloat16 or wider, within the bound.
A program may use at most 64 MiB of HBM per device.

v0:
```python
import jax
import jax.numpy as jnp
from jax import lax
from jax.sharding import PartitionSpec as P


def passed_along(block, axis, distance):
    devices = range(lax.axis_size(axis))
    route = [((i - distance) % len(devices), i) for i in devices]
    return lax.ppermute(block, axis, route)


def swish(values):
    return values * jax.nn.sigmoid(values)


def swish_slope(values):
    logistic = jax.nn.sigmoid(values)
    return logistic * (1.0 + values * (1.0 - logistic))


def contract_last(left, right):
    return lax.dot_general(
        left, right, (((1,), (1,)), ((), ())), preferred_element_type=jnp.float32
    )


def slot_plan(choice_ids, kept_flags, slot_index, weight_levels, experts_here, capacity):
    total_slots = experts_here * capacity
    target = jnp.where(kept_flags > 0, choice_ids * capacity + slot_index, total_slots).reshape(-1)
    source = jnp.broadcast_to(
        jnp.arange(choice_ids.shape[0], dtype=jnp.int32)[:, None], choice_ids.shape
    ).reshape(-1)
    slot_token = jnp.zeros((total_slots,), jnp.int32).at[target].set(source, mode="drop")
    levels = (weight_levels.astype(jnp.float32) / 4096.0).reshape(-1)
    slot_weight = jnp.zeros((total_slots,), jnp.float32).at[target].set(levels, mode="drop")
    slot_live = jnp.zeros((total_slots,), jnp.float32).at[target].set(1.0, mode="drop")
    return (slot_token, slot_weight, slot_live)


def section_link(values, offset):
    return passed_along(values, "pipe", offset)


def build_parcels(
    values_in, values_saved, values_cot, plan_forward, plan_backward, experts_here, capacity
):
    token_f, weight_f, live_f = plan_forward
    token_b, weight_b, live_b = plan_backward
    rows_in = jnp.where(live_f[:, None] > 0, values_in[token_f], jnp.zeros((), values_in.dtype))
    rows_saved = jnp.where(
        live_b[:, None] > 0, values_saved[token_b], jnp.zeros((), values_saved.dtype)
    )
    rows_cot = (weight_b[:, None] * values_cot[token_b].astype(jnp.float32)).astype(jnp.bfloat16)

    def doubled(rows):
        columns = rows.shape[-1]
        lined = rows.reshape(experts_here, 1, capacity, columns)
        spread = jnp.broadcast_to(lined, (experts_here, 2, capacity, columns))
        return spread.reshape(2 * experts_here, capacity, columns)

    return (doubled(rows_in), doubled(rows_saved), doubled(rows_cot))


def expert_local(rows_in, rows_saved, rows_cot, gate_w, up_w, down_w):
    gate_pre = jnp.dot(rows_in, gate_w, preferred_element_type=jnp.float32)
    up_pre = jnp.dot(rows_in, up_w, preferred_element_type=jnp.float32)
    hidden = (swish(gate_pre) * up_pre).astype(jnp.bfloat16)
    result = jnp.dot(hidden, down_w, preferred_element_type=jnp.float32).astype(jnp.bfloat16)
    gate_back = jnp.dot(rows_saved, gate_w, preferred_element_type=jnp.float32)
    up_back = jnp.dot(rows_saved, up_w, preferred_element_type=jnp.float32)
    grad_hidden = contract_last(rows_cot, down_w)
    grad_gate = (grad_hidden * up_back * swish_slope(gate_back)).astype(jnp.bfloat16)
    grad_up = (grad_hidden * swish(gate_back)).astype(jnp.bfloat16)
    grad_rows = (contract_last(grad_gate, gate_w) + contract_last(grad_up, up_w)).astype(
        jnp.bfloat16
    )
    return (result, grad_rows)


def shared_pass(full_in, full_saved, full_cot, gate_w, up_w, down_w):
    gate_pre = jnp.dot(full_in, gate_w, preferred_element_type=jnp.float32)
    up_pre = jnp.dot(full_in, up_w, preferred_element_type=jnp.float32)
    hidden = (swish(gate_pre) * up_pre).astype(jnp.bfloat16)
    shared_out = jnp.dot(hidden, down_w, preferred_element_type=jnp.float32)
    gate_back = jnp.dot(full_saved, gate_w, preferred_element_type=jnp.float32)
    up_back = jnp.dot(full_saved, up_w, preferred_element_type=jnp.float32)
    grad_hidden = contract_last(full_cot, down_w)
    grad_gate = (grad_hidden * up_back * swish_slope(gate_back)).astype(jnp.bfloat16)
    grad_up = (grad_hidden * swish(gate_back)).astype(jnp.bfloat16)
    shared_grad = contract_last(grad_gate, gate_w) + contract_last(grad_up, up_w)
    return (shared_out, shared_grad)


def local(
    inputs_prev,
    cotangent_next,
    saved_input,
    expert_ids,
    keep_mask,
    slot_pos,
    weight_q,
    gate_routed,
    up_routed,
    down_routed,
    gate_shared,
    up_shared,
    down_shared,
):
    capacity = inputs_prev.shape[1] // 32
    experts_here = lax.axis_size("expert") // 2
    forward_in = section_link(inputs_prev[0], 1)
    backward_in = section_link(cotangent_next[0], -1)
    saved_rows = saved_input[0]
    plan_forward = slot_plan(
        expert_ids[0, 0], keep_mask[0, 0], slot_pos[0, 0], weight_q[0, 0], experts_here, capacity
    )
    plan_backward = slot_plan(
        expert_ids[1, 0], keep_mask[1, 0], slot_pos[1, 0], weight_q[1, 0], experts_here, capacity
    )
    gate_w = gate_routed[0, 0]
    up_w = up_routed[0, 0]
    down_w = down_routed[0, 0]
    full_in, full_saved, full_cot = (
        lax.all_gather(forward_in, "tensor", axis=1, tiled=True),
        lax.all_gather(saved_rows, "tensor", axis=1, tiled=True),
        lax.all_gather(backward_in, "tensor", axis=1, tiled=True),
    )
    parcel_in, parcel_saved, parcel_cot = build_parcels(
        full_in, full_saved, full_cot, plan_forward, plan_backward, experts_here, capacity
    )
    pieces = (
        lax.all_to_all(parcel_in, "expert", split_axis=0, concat_axis=0, tiled=True),
        lax.all_to_all(parcel_saved, "expert", split_axis=0, concat_axis=0, tiled=True),
        lax.all_to_all(parcel_cot, "expert", split_axis=0, concat_axis=0, tiled=True),
    )
    row_shape = pieces[0].shape
    feature_count = row_shape[2]
    result, grad_rows = expert_local(
        pieces[0].reshape(-1, feature_count),
        pieces[1].reshape(-1, feature_count),
        pieces[2].reshape(-1, feature_count),
        gate_w,
        up_w,
        down_w,
    )
    returned = (
        lax.all_to_all(
            result.reshape(row_shape), "expert", split_axis=0, concat_axis=0, tiled=True
        ),
        lax.all_to_all(
            grad_rows.reshape(row_shape), "expert", split_axis=0, concat_axis=0, tiled=True
        ),
    )
    back_out, back_grad = returned
    feature_count = full_in.shape[1]
    merged_out = (
        back_out.astype(jnp.float32)
        .reshape(experts_here, 2, capacity, feature_count)
        .sum(axis=1)
        .reshape(experts_here * capacity, feature_count)
    )
    merged_grad = (
        back_grad.astype(jnp.float32)
        .reshape(experts_here, 2, capacity, feature_count)
        .sum(axis=1)
        .reshape(experts_here * capacity, feature_count)
    )
    token_f, weight_f, live_f = plan_forward
    token_b, weight_b, live_b = plan_backward
    routed_out = (
        jnp.zeros(full_in.shape, jnp.float32).at[token_f].add(weight_f[:, None] * merged_out)
    )
    routed_grad = (
        jnp.zeros(full_in.shape, jnp.float32).at[token_b].add(live_b[:, None] * merged_grad)
    )
    shared_out, shared_grad = shared_pass(
        full_in, full_saved, full_cot, gate_shared[0], up_shared[0], down_shared[0]
    )
    summed_out, summed_grad = (
        lax.psum_scatter(routed_out + shared_out, "tensor", scatter_dimension=1, tiled=True),
        lax.psum_scatter(routed_grad + shared_grad, "tensor", scatter_dimension=1, tiled=True),
    )
    return (summed_out.astype(jnp.bfloat16)[None], summed_grad.astype(jnp.bfloat16)[None])


def solution(mesh):
    return jax.shard_map(
        local,
        mesh=mesh,
        in_specs=(
            P("pipe", "expert", "tensor"),
            P("pipe", "expert", "tensor"),
            P("pipe", "expert", "tensor"),
            P(None, "pipe", "expert", None),
            P(None, "pipe", "expert", None),
            P(None, "pipe", "expert", None),
            P(None, "pipe", "expert", None),
            P("pipe", "expert", None, "tensor"),
            P("pipe", "expert", None, "tensor"),
            P("pipe", "expert", "tensor", None),
            P("pipe", None, "tensor"),
            P("pipe", None, "tensor"),
            P("pipe", "tensor", None),
        ),
        out_specs=(P("pipe", "expert", "tensor"), P("pipe", "expert", "tensor")),
        check_vma=False,
    )
```

profile of v0, /device:TPU:0, one launch (start us, length us, event | category | flops | bytes accessed | tf_op | source)
XLA Modules:
  0.0 146.0 jit_solution(13066194130727708834)
XLA Ops:
  7.2 0.9 add_select_fusion
  8.1 0.1 copy.17
  8.2 0.1 select_n.83
  8.3 0.1 reshape.298
  8.4 4.3 %scatter_custom_fusion.4 = s32[8]{0:T(128)S(1)} fusion(s32[1024]{0:T(1024)S(1)} %bitcast.104, s32[1024]{0:T(1024)S(1)} %reshape.298, s32[]{:T(128)} %constant.9.clone.1), kind=kCustom, calls=%fused_computation.111 | custom fusion | bytes 36 | tf_op jit(solution)/shard_map/scatter | solution.py:34
  12.7 2.8 %all-gather = bf16[1,128,3584]{2,1,0:T(8,128)(2,1)S(1)} all-gather(bf16[1,128,1792]{2,1,0:T(8,128)(2,1)} %param.15), channel_id=2, replica_groups=mesh['pipe'=4,'expert'=4,'tensor'=2] {'tensor'}, dimensions={2}, use_global_device_ids=true | all-gather | bytes 1376256 | tf_op jit(solution)/shard_map/all_gather | solution.py:126
  15.5 0.6 gather_fusion.2
  16.2 4.3 %scatter_custom_fusion.5 = f32[8]{0:T(128)S(1)} fusion(s32[1024]{0:T(1024)S(1)} %bitcast.105, f32[1024]{0:T(1024)S(1)} %broadcast.165, f32[]{:T(128)} %constant.13.clone.1), kind=kCustom, calls=%fused_computation.104 | custom fusion | bytes 36 | tf_op jit(solution)/shard_map/scatter | solution.py:37
  20.5 0.1 broadcast_in_dim.93
  20.6 0.1 broadcast_select_fusion
  20.7 0.7 broadcast_in_dim.95
  21.4 5.1 %all-to-all-start.3 = ((bf16[4,4,3584]{2,1,0:T(4,128)(2,1)}), bf16[4,4,3584]{2,1,0:T(4,128)(2,1)S(1)}, u32[]{:S(2)}, u32[]{:S(2)}) async-start(bf16[4,4,3584]{2,1,0:T(4,128)(2,1)} %bitcast.15), calls=%async_computation.4 | async-start | bytes 229376 | tf_op jit(solution)/shard_map/all_to_all | solution.py:134
  26.4 3.6 %collective-permute-start.1 = (bf16[128,1792]{1,0:T(8,128)(2,1)}, bf16[128,1792]{1,0:T(8,128)(2,1)}, u32[]{:S(2)}, u32[]{:S(2)}) collective-permute-start(bf16[128,1792]{1,0:T(8,128)(2,1)} %bitcast.110), channel_id=1, source_target_pairs={{8,0},{16,8},{24,16},{0,24},{9,1},{17,9},{25,17},{1,25},{10,2},{18... | collective-permute-start | bytes 1376264 | tf_op jit(solution)/shard_map/ppermute | solution.py:10
  30.0 2.7 %fusion.12 = f32[128,512]{1,0:T(8,128)S(1)} fusion(bf16[1,3584,512]{2,1,0:T(8,128)(2,1)} %param.23, bf16[1,128,3584]{2,1,0:T(8,128)(2,1)S(1)} %all-gather), kind=kOutput, calls=%fused_computation.26 | convolution fusion | flops 469762048 | bytes 4849664 | tf_op jit(solution)/shard_map/dot_general | solution.py:86
  32.7 0.1 copy.18
  32.8 0.1 reshape.314
  32.9 4.3 %scatter_custom_fusion.6 = f32[8]{0:T(128)S(1)} fusion(s32[1024]{0:T(1024)S(1)} %bitcast.106, f32[1024]{0:T(1024)S(1)} %reshape.314, f32[]{:T(128)} %constant.13.clone.1), kind=kCustom, calls=%fused_computation.102 | custom fusion | bytes 36 | tf_op jit(solution)/shard_map/scatter | solution.py:36
  37.2 0.1 mul.117
  37.4 1.8 %fusion.26 = f32[16,256]{1,0:T(8,128)S(1)} fusion(bf16[16,3584]{1,0:T(8,128)(2,1)S(1)} %reshape.228, bf16[1,1,3584,256]{3,2,1,0:T(8,128)(2,1)} %param.20), kind=kOutput, calls=%fused_computation.40 | convolution fusion | flops 29360128 | bytes 1966080 | tf_op jit(solution)/shard_map/dot_general | solution.py:70
  39.2 0.9 collective-permute-done.1
  40.1 4.2 %all_gather.10 = bf16[128,3584]{1,0:T(8,128)(2,1)} all-gather(bf16[128,1792]{1,0:T(8,128)(2,1)} %collective-permute-done.1), channel_id=1, replica_groups=mesh['pipe'=4,'expert'=4,'tensor'=2] {'tensor'}, dimensions={1}, use_global_device_ids=true | all-gather | bytes 1376256 | tf_op jit(solution)/shard_map/all_gather | solution.py:127
  44.3 1.9 %gather_fusion.1 = bf16[8,3584]{1,0:T(8,128)(2,1)S(1)} fusion(bf16[128,3584]{1,0:T(8,128)(2,1)} %all_gather.10, s32[1024]{0:T(1024)S(1)} %pad_clamp_fusion), kind=kCustom, calls=%fused_computation.1 | custom fusion | bytes 114720 | tf_op jit(solution)/shard_map/gather | solution.py:54
  46.3 0.1 multiply_convert_fusion.4
  46.4 0.7 broadcast_in_dim.92
  47.1 3.9 %all-to-all-start.2 = ((bf16[4,4,3584]{2,1,0:T(4,128)(2,1)}), bf16[4,4,3584]{2,1,0:T(4,128)(2,1)S(1)}, u32[]{:S(2)}, u32[]{:S(2)}) async-start(bf16[4,4,3584]{2,1,0:T(4,128)(2,1)} %bitcast.14), calls=%async_computation.3 | async-start | bytes 229376 | tf_op jit(solution)/shard_map/all_to_all | solution.py:135
  51.0 3.6 %fusion.1 = f32[128,512]{1,0:T(8,128)S(1)} fusion(bf16[128,3584]{1,0:T(8,128)(2,1)} %all_gather.10, bf16[1,512,3584]{2,1,0:T(8,128)(2,1)} %param.25), kind=kOutput, calls=%fused_computation.15 | convolution fusion | flops 469762048 | bytes 4849664 | tf_op jit(solution)/shard_map/dot_general | solution.py:23
  54.6 6.2 %fusion.10 = f32[128,3584]{1,0:T(8,128)} fusion(bf16[1,3584,512]{2,1,0:T(8,128)(2,1)} %param.23, f32[128,512]{1,0:T(8,128)S(1)} %fusion.1, bf16[1,3584,512]{2,1,0:T(8,128)(2,1)} %param.24, f32[128,512]{1,0:T(8,128)S(1)} %fusion.12, bf16[1,128,3584]{2,1,0:T(8,128)(2,1)S(1)} %all-gather), kind=kOutput, calls=%fused_computation.24 | convolution fusion | flops 940179456 | bytes 10616832 | tf_op jit(solution)/shard_map/dot_general | solution.py:23
  60.9 2.1 %fusion.16 = f32[16,256]{1,0:T(8,128)S(1)} fusion(bf16[16,3584]{1,0:T(8,128)(2,1)S(1)} %reshape.226, bf16[1,1,256,3584]{3,2,1,0:T(8,128)(2,1)} %param.22), kind=kOutput, calls=%fused_computation.30 | convolution fusion | flops 29360128 | bytes 1966080 | tf_op jit(solution)/shard_map/dot_general | solution.py:23
  63.0 2.8 %fusion.24 = f32[16,3584]{1,0:T(8,128)S(1)} fusion(bf16[1,1,3584,256]{3,2,1,0:T(8,128)(2,1)} %param.20, f32[16,256]{1,0:T(8,128)S(1)} %fusion.16, bf16[16,3584]{1,0:T(8,128)(2,1)S(1)} %reshape.228, bf16[1,1,3584,256]{3,2,1,0:T(8,128)(2,1)S(1)} %copy-done, f32[16,256]{1,0:T(8,128)S(1)} %fusion.26), kind=kOutput, calls=%fused_computation.38 | convolution fusion | flops 58761216 | bytes 4046848 | tf_op jit(solution)/shard_map/dot_general | solution.py:23
  65.8 0.6 fusion
  66.4 0.7 reshape.229
  67.1 4.2 %all-to-all-start.4 = ((bf16[4,4,3584]{2,1,0:T(4,128)(2,1)}), bf16[4,4,3584]{2,1,0:T(4,128)(2,1)S(1)}, u32[]{:S(2)}, u32[]{:S(2)}) async-start(bf16[4,4,3584]{2,1,0:T(4,128)(2,1)} %reshape.229), calls=%async_computation.5 | async-start | bytes 229376 | tf_op jit(solution)/shard_map/all_to_all | solution.py:151
  71.3 5.2 %convolution_add_fusion = f32[128,3584]{1,0:T(8,128)} fusion(f32[128,3584]{1,0:T(8,128)} %fusion.10, bf16[1,3584,512]{2,1,0:T(8,128)(2,1)} %param.24, f32[128,512]{1,0:T(8,128)S(1)} %fusion.1, f32[128,512]{1,0:T(8,128)S(1)} %fusion.12), kind=kOutput, calls=%fused_computation.11 | convolution fusion | flops 470614016 | bytes 7864320 | tf_op jit(solution)/shard_map/dot_general | solution.py:23
  76.4 0.1 convert_reduce_fusion
  76.6 3.6 %scatter_custom_fusion.7 = f32[128,3584]{1,0:T(8,128)} fusion(f32[128,3584]{1,0:T(8,128)} %convolution_add_fusion, s32[8]{0:T(128)S(1)} %compare_select_fusion.2, f32[8,3584]{1,0:T(8,128)S(1)} %reshape.232, f32[8]{0:T(128)S(1)} %scatter_custom_fusion.5), kind=kCustom, calls=%fused_computation.66 | custom fusion | flops 57344 | bytes 1950208 | tf_op jit(solution)/shard_map/scatter-add | solution.py:175
  80.2 0.5 collective-permute-start
  80.7 0.1 copy.15
  80.8 0.1 select_n.78
  80.9 4.3 %scatter_custom_fusion = s32[8]{0:T(128)S(1)} fusion(s32[1024]{0:T(1024)S(1)} %bitcast.107, s32[1024]{0:T(1024)S(1)} %reshape.298, s32[]{:T(128)} %constant.9.clone.1), kind=kCustom, calls=%fused_computation.113 | custom fusion | bytes 36 | tf_op jit(solution)/shard_map/scatter | solution.py:34
  85.2 4.5 %scatter_custom_fusion.2 = f32[8]{0:T(128)S(1)} fusion(s32[1024]{0:T(1024)S(1)} %bitcast.108, f32[1024]{0:T(1024)S(1)} %broadcast.165, f32[]{:T(128)} %constant.13.clone.1), kind=kCustom, calls=%fused_computation.107 | custom fusion | bytes 36 | tf_op jit(solution)/shard_map/scatter | solution.py:37
  89.7 0.1 broadcast_in_dim.86
  89.8 0.1 copy.16
  89.9 0.1 reshape.274
  90.0 4.3 %scatter_custom_fusion.1 = f32[8]{0:T(128)S(1)} fusion(s32[1024]{0:T(1024)S(1)} %bitcast.109, f32[1024]{0:T(1024)S(1)} %reshape.274, f32[]{:T(128)} %constant.13.clone.1), kind=kCustom, calls=%fused_computation.109 | custom fusion | bytes 36 | tf_op jit(solution)/shard_map/scatter | solution.py:36
  94.3 0.4 collective-permute-done
  94.7 2.5 %all_gather.9 = bf16[128,3584]{1,0:T(8,128)(2,1)S(1)} all-gather(bf16[128,1792]{1,0:T(8,128)(2,1)S(1)} %collective-permute-done), channel_id=1, replica_groups=mesh['pipe'=4,'expert'=4,'tensor'=2] {'tensor'}, dimensions={1}, use_global_device_ids=true | all-gather | bytes 1376256 | tf_op jit(solution)/shard_map/all_gather | solution.py:125
  97.2 0.6 gather_fusion
  97.8 0.1 broadcast_select_fusion.1
  97.9 0.7 broadcast_in_dim.89
  98.6 3.9 %all-to-all-start = ((bf16[4,4,3584]{2,1,0:T(4,128)(2,1)}), bf16[4,4,3584]{2,1,0:T(4,128)(2,1)S(1)}, u32[]{:S(2)}, u32[]{:S(2)}) async-start(bf16[4,4,3584]{2,1,0:T(4,128)(2,1)} %bitcast.5), calls=%async_computation | async-start | bytes 229376 | tf_op jit(solution)/shard_map/all_to_all | solution.py:133
  102.5 2.7 %fusion.8 = f32[128,512]{1,0:T(8,128)S(1)} fusion(bf16[128,3584]{1,0:T(8,128)(2,1)S(1)} %all_gather.9, bf16[1,3584,512]{2,1,0:T(8,128)(2,1)} %param.24), kind=kOutput, calls=%fused_computation.22 | convolution fusion | flops 469762048 | bytes 4849664 | tf_op jit(solution)/shard_map/dot_general | solution.py:83
  105.2 2.3 %all-to-all-done = bf16[4,4,3584]{2,1,0:T(4,128)(2,1)S(1)} async-done(((bf16[4,4,3584]{2,1,0:T(4,128)(2,1)}), bf16[4,4,3584]{2,1,0:T(4,128)(2,1)S(1)}, u32[]{:S(2)}, u32[]{:S(2)}) %all-to-all-start) | async-done | bytes 114720 | tf_op jit(solution)/shard_map/all_to_all | solution.py:133
  107.5 1.8 %fusion.28 = f32[16,256]{1,0:T(8,128)S(1)} fusion(bf16[16,3584]{1,0:T(8,128)(2,1)S(1)} %reshape.220, bf16[1,1,3584,256]{3,2,1,0:T(8,128)(2,1)} %param.20), kind=kOutput, calls=%fused_computation.42 | convolution fusion | flops 29360128 | bytes 1966080 | tf_op jit(solution)/shard_map/dot_general | solution.py:66
  109.3 2.6 %convolution_convert_fusion = bf16[16,3584]{1,0:T(8,128)(2,1)S(1)} fusion(bf16[1,1,256,3584]{3,2,1,0:T(8,128)(2,1)} %param.22, bf16[16,3584]{1,0:T(8,128)(2,1)S(1)} %reshape.220, bf16[1,1,3584,256]{3,2,1,0:T(8,128)(2,1)S(1)} %copy-done, f32[16,256]{1,0:T(8,128)S(1)} %fusion.28), kind=kOutput, calls=%fused_computation.14 | convolution fusion | flops 58802176 | bytes 3915776 | tf_op jit(solution)/shard_map/dot_general | solution.py:69
  112.0 0.7 reshape.221
  112.7 3.3 %all-to-all-start.1 = ((bf16[4,4,3584]{2,1,0:T(4,128)(2,1)}), bf16[4,4,3584]{2,1,0:T(4,128)(2,1)S(1)}, u32[]{:S(2)}, u32[]{:S(2)}) async-start(bf16[4,4,3584]{2,1,0:T(4,128)(2,1)} %reshape.221), calls=%async_computation.1 | async-start | bytes 229376 | tf_op jit(solution)/shard_map/all_to_all | solution.py:148
  116.0 0.0 reduce-scatter.3.cloned.1.call-start
  116.0 5.7 %fusion.3 = f32[128,3584]{1,0:T(8,128)} fusion(bf16[1,512,3584]{2,1,0:T(8,128)(2,1)} %param.25, f32[128,512]{1,0:T(8,128)S(1)} %fusion.8, bf16[128,3584]{1,0:T(8,128)(2,1)S(1)} %all_gather.9, bf16[1,3584,512]{2,1,0:T(8,128)(2,1)} %param.23), kind=kOutput, calls=%fused_computation.17 | convolution fusion | flops 939917312 | bytes 10354688 | tf_op jit(solution)/shard_map/dot_general | solution.py:85
  121.7 0.1 convert_reduce_fusion.1
  121.8 3.5 %scatter_custom_fusion.3 = f32[128,3584]{1,0:T(8,128)} fusion(f32[128,3584]{1,0:T(8,128)} %fusion.3, s32[8]{0:T(128)S(1)} %compare_select_fusion.3, f32[8,3584]{1,0:T(8,128)S(1)} %reshape.224, f32[8]{0:T(128)S(1)} %scatter_custom_fusion.1), kind=kCustom, calls=%fused_computation.69 | custom fusion | flops 57344 | bytes 1950208 | tf_op jit(solution)/shard_map/scatter-add | solution.py:172
  125.4 0.0 reduce-scatter.5.cloned.1.call-done
  125.4 2.0 %convert_bitcast_fusion = bf16[1,128,1792]{2,1,0:T(8,128)(2,1)} fusion(f32[128,1792]{1,0:T(8,128)} %reduce-scatter.5.cloned.1.call-done), kind=kLoop, calls=%fused_computation.52 | loop fusion | flops 229376 | bytes 1376256 | tf_op jit(solution)/shard_map/broadcast_in_dim | solution.py:184
  127.4 9.8 %reduce-scatter.3.cloned.1.call-done = f32[128,1792]{1,0:T(8,128)} async-done(((f32[128,3584]{1,0:T(8,128)}), f32[128,1792]{1,0:T(8,128)}) %reduce-scatter.3.cloned.1.call-update) | async-done | bytes 917520 | tf_op jit(solution)/shard_map/reduce_scatter | solution.py:181
  137.2 2.0 %convert_bitcast_fusion.1 = bf16[1,128,1792]{2,1,0:T(8,128)(2,1)} fusion(f32[128,1792]{1,0:T(8,128)} %reduce-scatter.3.cloned.1.call-done), kind=kLoop, calls=%fused_computation.53 | loop fusion | flops 229376 | bytes 1376256 | tf_op jit(solution)/shard_map/broadcast_in_dim | solution.py:184
  (32 shorter events, 0.4 us)
Async XLA Ops:
  7.2 55.8 %copy-start = (bf16[1,1,3584,256]{3,2,1,0:T(8,128)(2,1)S(1)}, bf16[1,1,3584,256]{3,2,1,0:T(8,128)(2,1)}, u32[]{:S(2)}) copy-start(bf16[1,1,3584,256]{3,2,1,0:T(8,128)(2,1)} %param.21) | copy-start | bytes 5505028
  21.4 16.0 %all-to-all-start.3 = ((bf16[4,4,3584]{2,1,0:T(4,128)(2,1)}), bf16[4,4,3584]{2,1,0:T(4,128)(2,1)S(1)}, u32[]{:S(2)}, u32[]{:S(2)}) async-start(bf16[4,4,3584]{2,1,0:T(4,128)(2,1)} %bitcast.15), calls=%async_computation.4 | async-start | bytes 229376 | tf_op jit(solution)/shard_map/all_to_all | solution.py:134
  26.4 6.3 %copy-start.1 = (s32[2,1,128,8]{2,3,1,0:T(8,128)S(1)}, s32[2,1,128,8]{2,3,1,0:T(8,128)}, u32[]{:S(2)}) copy-start(s32[2,1,128,8]{2,3,1,0:T(8,128)} %param.19) | copy-start | bytes 24580
  26.4 13.7 %collective-permute-start.1 = (bf16[128,1792]{1,0:T(8,128)(2,1)}, bf16[128,1792]{1,0:T(8,128)(2,1)}, u32[]{:S(2)}, u32[]{:S(2)}) collective-permute-start(bf16[128,1792]{1,0:T(8,128)(2,1)} %bitcast.110), channel_id=1, source_target_pairs={{8,0},{16,8},{24,16},{0,24},{9,1},{17,9},{25,17},{1,25},{10,2},{18... | collective-permute-start | bytes 1376264 | tf_op jit(solution)/shard_map/ppermute | solution.py:10
  47.1 13.8 %all-to-all-start.2 = ((bf16[4,4,3584]{2,1,0:T(4,128)(2,1)}), bf16[4,4,3584]{2,1,0:T(4,128)(2,1)S(1)}, u32[]{:S(2)}, u32[]{:S(2)}) async-start(bf16[4,4,3584]{2,1,0:T(4,128)(2,1)} %bitcast.14), calls=%async_computation.3 | async-start | bytes 229376 | tf_op jit(solution)/shard_map/all_to_all | solution.py:135
  67.1 9.4 %all-to-all-start.4 = ((bf16[4,4,3584]{2,1,0:T(4,128)(2,1)}), bf16[4,4,3584]{2,1,0:T(4,128)(2,1)S(1)}, u32[]{:S(2)}, u32[]{:S(2)}) async-start(bf16[4,4,3584]{2,1,0:T(4,128)(2,1)} %reshape.229), calls=%async_computation.5 | async-start | bytes 229376 | tf_op jit(solution)/shard_map/all_to_all | solution.py:151
  71.3 54.1 %reduce-scatter.5.cloned.1.call-start = ((), (), s32[]{:S(2)}) async-start(), calls=%async_computation.8 | async-start | bytes 2752512 | tf_op jit(solution)/shard_map/reduce_scatter | solution.py:182
  76.6 3.6 %copy-start.2 = (bf16[1,128,1792]{2,1,0:T(8,128)(2,1)S(1)}, bf16[1,128,1792]{2,1,0:T(8,128)(2,1)}, u32[]{:S(2)}) copy-start(bf16[1,128,1792]{2,1,0:T(8,128)(2,1)} %param.13) | copy-start | bytes 1376260
  80.2 14.6 %collective-permute-start = (bf16[128,1792]{1,0:T(8,128)(2,1)S(1)}, bf16[128,1792]{1,0:T(8,128)(2,1)S(1)}, u32[]{:S(2)}, u32[]{:S(2)}) collective-permute-start(bf16[128,1792]{1,0:T(8,128)(2,1)S(1)} %bitcast.111), channel_id=1, source_target_pairs={{24,0},{0,8},{8,16},{16,24},{25,1},{1,9},{9,17},{17,25},{26,2},{2,... | collective-permute-start | bytes 1376264 | tf_op jit(solution)/shard_map/ppermute | solution.py:10
  98.6 8.9 %all-to-all-start = ((bf16[4,4,3584]{2,1,0:T(4,128)(2,1)}), bf16[4,4,3584]{2,1,0:T(4,128)(2,1)S(1)}, u32[]{:S(2)}, u32[]{:S(2)}) async-start(bf16[4,4,3584]{2,1,0:T(4,128)(2,1)} %bitcast.5), calls=%async_computation | async-start | bytes 229376 | tf_op jit(solution)/shard_map/all_to_all | solution.py:133
  112.7 9.1 %all-to-all-start.1 = ((bf16[4,4,3584]{2,1,0:T(4,128)(2,1)}), bf16[4,4,3584]{2,1,0:T(4,128)(2,1)S(1)}, u32[]{:S(2)}, u32[]{:S(2)}) async-start(bf16[4,4,3584]{2,1,0:T(4,128)(2,1)} %reshape.221), calls=%async_computation.1 | async-start | bytes 229376 | tf_op jit(solution)/shard_map/all_to_all | solution.py:148
  116.0 21.2 %reduce-scatter.3.cloned.1.call-start = ((), (), s32[]{:S(2)}) async-start(), calls=%async_computation.7 | async-start | bytes 2752512 | tf_op jit(solution)/shard_map/reduce_scatter | solution.py:181
Sparse Core Ops, SparseCore 0:
  80.3 11.7 reduce-scatter.4
  125.5 11.6 reduce-scatter.2
where the time goes:
time: 147 us; the launch traced here: 146 us
  matrix products  37.8 us (26%)
  local copies, waits for them, and re-layouts  34 us (23%)
  starting transfers between devices  24.6 us (17%)
  between operations  14.3 us (10%)
  waiting for transfers between devices  13.5 us (9%)
  other arithmetic  12.4 us (8%)
  blocking collectives  9.43 us (6%)
    dot_general x6, matrix products, contract_last(): lax.dot_general(left, right, (((1,), (1,)), ((), ())), preferred_element_...  20.5 us
    reduce_scatter x1, waiting for transfers between devices, local(): lax.psum_scatter(routed_out + shared_out, 'tensor', scatter_dimension=1,...  9.78 us
    scatter x2, local copies, waits for them, and re-layouts, slot_plan(): jnp.zeros((total_slots,), jnp.float32).at[target].set(1.0, mode='drop')  8.79 us
    scatter x2, local copies, waits for them, and re-layouts, slot_plan(): jnp.zeros((total_slots,), jnp.int32).at[target].set(source, mode='drop')  8.61 us
    scatter x2, local copies, waits for them, and re-layouts, slot_plan(): jnp.zeros((total_slots,), jnp.float32).at[target].set(levels, mode='drop')  8.61 us
    dot_general x1, matrix products, shared_pass(): shared_out = jnp.dot(hidden, down_w, preferred_element_type=jnp.float32)  5.68 us
    all_to_all x1, starting transfers between devices, local(): lax.all_to_all(parcel_saved, 'expert', split_axis=0, concat_axis=0, tiled...  5.07 us
    all_to_all x1, starting transfers between devices, local(): lax.all_to_all(grad_rows.reshape(row_shape), 'expert', split_axis=0, conc...  4.19 us
  transfers between devices with their start and end apart: 9, of which 4 were waited for; matrix products, arithmetic and copies ran while one was open for 40% of the time, Pallas kernels for 0%

commit v1 on v0

v1 whole, which is shorter than its diff:
```python
import jax
import jax.numpy as jnp
from jax import lax
from jax.sharding import PartitionSpec as P


def passed_along(block, axis, distance):
    devices = range(lax.axis_size(axis))
    route = [((i - distance) % len(devices), i) for i in devices]
    return lax.ppermute(block, axis, route)


def swish(values):
    return values * jax.nn.sigmoid(values)


def swish_slope(values):
    logistic = jax.nn.sigmoid(values)
    return logistic * (1.0 + values * (1.0 - logistic))


def contract_last(left, right):
    return lax.dot_general(
        left, right, (((1,), (1,)), ((), ())), preferred_element_type=jnp.float32
    )


def slot_plan(choice_ids, kept_flags, slot_index, weight_levels, total_slots, capacity):
    target = jnp.where(kept_flags > 0, choice_ids * capacity + slot_index, -1)
    slots = jnp.arange(total_slots, dtype=jnp.int32)
    match = target[None] == slots[:, None, None]
    chosen = jnp.sum(match.astype(jnp.int32), axis=2)
    level = jnp.sum(jnp.where(match, weight_levels[None], 0), axis=2)
    return chosen.astype(jnp.bfloat16), level


def section_link(values, offset):
    return passed_along(values, "pipe", offset)


def select_rows(chosen, values):
    return jnp.dot(chosen, values, preferred_element_type=jnp.float32)


def split_level(level):
    high = (level // 64).astype(jnp.float32) / 64.0
    low = (level % 64).astype(jnp.float32) / 4096.0
    return high.astype(jnp.bfloat16), low.astype(jnp.bfloat16)


def combine(factors, rows):
    return lax.dot_general(
        factors, rows, (((0,), (0,)), ((), ())), preferred_element_type=jnp.float32
    )


def other_sums(total, n_tensor):
    width = total.shape[1] // n_tensor
    me = lax.axis_index("tensor")
    mine = lax.dynamic_slice_in_dim(total, me * width, width, axis=1)
    for step in range(1, n_tensor):
        to = (me + step) % n_tensor
        piece = lax.dynamic_slice_in_dim(total, to * width, width, axis=1)
        mine = mine + passed_along(piece, "tensor", step)
    return mine


def expert_local(rows_in, rows_saved, rows_cot, gate_w, up_w, down_w):
    gate_pre = jnp.dot(rows_in, gate_w, preferred_element_type=jnp.float32)
    up_pre = jnp.dot(rows_in, up_w, preferred_element_type=jnp.float32)
    hidden = (swish(gate_pre) * up_pre).astype(jnp.bfloat16)
    result = jnp.dot(hidden, down_w, preferred_element_type=jnp.float32).astype(jnp.bfloat16)
    gate_back = jnp.dot(rows_saved, gate_w, preferred_element_type=jnp.float32)
    up_back = jnp.dot(rows_saved, up_w, preferred_element_type=jnp.float32)
    grad_hidden = contract_last(rows_cot, down_w)
    grad_gate = (grad_hidden * up_back * swish_slope(gate_back)).astype(jnp.bfloat16)
    grad_up = (grad_hidden * swish(gate_back)).astype(jnp.bfloat16)
    grad_rows = (contract_last(grad_gate, gate_w) + contract_last(grad_up, up_w)).astype(
        jnp.bfloat16
    )
    return (result, grad_rows)


def shared_pass(full_in, full_saved, full_cot, gate_w, up_w, down_w):
    gate_pre = jnp.dot(full_in, gate_w, preferred_element_type=jnp.float32)
    up_pre = jnp.dot(full_in, up_w, preferred_element_type=jnp.float32)
    hidden = (swish(gate_pre) * up_pre).astype(jnp.bfloat16)
    shared_out = jnp.dot(hidden, down_w, preferred_element_type=jnp.float32)
    gate_back = jnp.dot(full_saved, gate_w, preferred_element_type=jnp.float32)
    up_back = jnp.dot(full_saved, up_w, preferred_element_type=jnp.float32)
    grad_hidden = contract_last(full_cot, down_w)
    grad_gate = (grad_hidden * up_back * swish_slope(gate_back)).astype(jnp.bfloat16)
    grad_up = (grad_hidden * swish(gate_back)).astype(jnp.bfloat16)
    shared_grad = contract_last(grad_gate, gate_w) + contract_last(grad_up, up_w)
    return (shared_out, shared_grad)


def local(
    inputs_prev,
    cotangent_next,
    saved_input,
    expert_ids,
    keep_mask,
    slot_pos,
    weight_q,
    gate_routed,
    up_routed,
    down_routed,
    gate_shared,
    up_shared,
    down_shared,
):
    capacity = inputs_prev.shape[1] // 32
    n_expert = lax.axis_size("expert")
    n_tensor = lax.axis_size("tensor")
    experts_here = n_expert // 2
    slots = experts_here * capacity
    forward_in = section_link(inputs_prev[0], 1)
    backward_in = section_link(cotangent_next[0], -1)
    chosen_f, level_f = slot_plan(
        expert_ids[0, 0], keep_mask[0, 0], slot_pos[0, 0], weight_q[0, 0], slots, capacity
    )
    chosen_b, level_b = slot_plan(
        expert_ids[1, 0], keep_mask[1, 0], slot_pos[1, 0], weight_q[1, 0], slots, capacity
    )
    gate_w = gate_routed[0, 0]
    up_w = up_routed[0, 0]
    down_w = down_routed[0, 0]
    full_saved = lax.all_gather(saved_input[0], "tensor", axis=1, tiled=True)
    full_in = lax.all_gather(forward_in, "tensor", axis=1, tiled=True)
    full_cot = lax.all_gather(backward_in, "tensor", axis=1, tiled=True)
    feature_count = full_in.shape[1]
    weight_b = jnp.sum(level_b, axis=1).astype(jnp.float32) / 4096.0
    parcel = jnp.stack(
        (
            select_rows(chosen_f, full_in).astype(jnp.bfloat16),
            select_rows(chosen_b, full_saved).astype(jnp.bfloat16),
            (weight_b[:, None] * select_rows(chosen_b, full_cot)).astype(jnp.bfloat16),
        )
    ).reshape(3, experts_here, 1, capacity, feature_count)
    parcel = jnp.broadcast_to(parcel, (3, experts_here, 2, capacity, feature_count))
    parcel = parcel.reshape(3, n_expert, capacity, feature_count)
    pieces = lax.all_to_all(parcel, "expert", split_axis=1, concat_axis=1, tiled=True)
    rows = pieces.reshape(3, n_expert * capacity, feature_count)
    result, grad_rows = expert_local(rows[0], rows[1], rows[2], gate_w, up_w, down_w)
    returned = lax.all_to_all(
        jnp.stack((result, grad_rows)).reshape(2, n_expert, capacity, feature_count),
        "expert", split_axis=1, concat_axis=1, tiled=True,
    )
    back = returned.reshape(2, n_expert * capacity, feature_count)

    def doubled(factors):
        spread = factors.reshape(experts_here, 1, capacity, -1)
        spread = jnp.broadcast_to(spread, (experts_here, 2) + spread.shape[2:])
        return spread.reshape(n_expert * capacity, -1)

    high_f, low_f = split_level(level_f)
    factors_f = jnp.concatenate((doubled(high_f), doubled(low_f)), axis=0)
    routed_out = combine(factors_f, jnp.concatenate((back[0], back[0]), axis=0))
    routed_grad = combine(doubled(chosen_b), back[1])
    shared_out, shared_grad = shared_pass(
        full_in, full_saved, full_cot, gate_shared[0], up_shared[0], down_shared[0]
    )
    summed_out = other_sums(routed_out + shared_out, n_tensor)
    summed_grad = other_sums(routed_grad + shared_grad, n_tensor)
    return (summed_out.astype(jnp.bfloat16)[None], summed_grad.astype(jnp.bfloat16)[None])


def solution(mesh):
    return jax.shard_map(
        local,
        mesh=mesh,
        in_specs=(
            P("pipe", "expert", "tensor"),
            P("pipe", "expert", "tensor"),
            P("pipe", "expert", "tensor"),
            P(None, "pipe", "expert", None),
            P(None, "pipe", "expert", None),
            P(None, "pipe", "expert", None),
            P(None, "pipe", "expert", None),
            P("pipe", "expert", None, "tensor"),
            P("pipe", "expert", None, "tensor"),
            P("pipe", "expert", "tensor", None),
            P("pipe", None, "tensor"),
            P("pipe", None, "tensor"),
            P("pipe", "tensor", None),
        ),
        out_specs=(P("pipe", "expert", "tensor"), P("pipe", "expert", "tensor")),
        check_vma=False,
    )
```

time: 147 us -> 101 us (0.69)
  local copies, waits for them, and re-layouts: 34 us -> 15.7 us
  between operations: 14.3 us -> 0.82 us
  starting transfers between devices: 24.6 us -> 13.9 us
  other arithmetic: 12.4 us -> 7.08 us
  matrix products: 37.8 us -> 42.3 us
  blocking collectives: 9.43 us -> 7.79 us
    scatter x6 -> x0, local copies, waits for them, and re-layouts: 26 us -> none  [the longest x2 8.79 us: slot_plan(): jnp.zeros((total_slots,), jnp.float32).at[target].set(1.0, mode='drop')]
    all_to_all x5 -> x2, starting transfers between devices: 20.4 us -> 8.25 us  [the longest x1 4.14 us: local(): lax.all_to_all(jnp.stack((result, grad_rows)).reshape(2, n_expert, capaci...]
    reduce_scatter x2 -> x0, waiting for transfers between devices: 9.8 us -> none  [the longest x1 9.78 us: local(): lax.psum_scatter(routed_out + shared_out, 'tensor', scatter_dimension=1,...]
    ppermute x2 -> x4, waiting for transfers between devices: 1.33 us -> 9.2 us  [passed_along(): return lax.ppermute(block, axis, route)]
    scatter-add x2 -> x0, other arithmetic: 7.05 us -> none  [the longest x1 3.57 us: local(): jnp.zeros(full_in.shape, jnp.float32).at[token_b]]
    dot_general x0 -> x5, matrix products: none -> 4.41 us  [the longest x2 3.06 us: combine(): lax.dot_general(factors, rows, (((0,), (0,)), ((), ())), preferred_elemen...]
    slice x0 -> x2, local copies, waits for them, and re-layouts: none -> 3.49 us  [the longest x1 1.77 us: local(): rows[0]]
    squeeze x0 -> x5, local copies, waits for them, and re-layouts: none -> 3.24 us  [the longest x1 1.57 us: local(): routed_out = combine(factors_f, jnp.concatenate((back[0], back[0]), axis=0))]
  transfers between devices with their start and end apart: 9 -> 6, of which waited for: 4 -> 4; matrix products, arithmetic and copies ran while one was open for 40% -> 26% of each run, Pallas kernels for 0% -> 0%
where the time goes in v1:
time: 101 us; the launch traced here: 99.7 us
  matrix products  42.3 us (42%)
  local copies, waits for them, and re-layouts  15.7 us (16%)
  starting transfers between devices  13.9 us (14%)
  waiting for transfers between devices  12.2 us (12%)
  blocking collectives  7.79 us (8%)
  other arithmetic  7.08 us (7%)
    dot_general x6, matrix products, contract_last(): lax.dot_general(left, right, (((1,), (1,)), ((), ())), preferred_element_...  20.8 us
    ppermute x4, waiting for transfers between devices, passed_along(): return lax.ppermute(block, axis, route)  9.2 us
    dot_general x1, matrix products, shared_pass(): shared_out = jnp.dot(hidden, down_w, preferred_element_type=jnp.float32)  6.2 us
    ppermute x4, starting transfers between devices, passed_along(): return lax.ppermute(block, axis, route)  5.64 us
    all_to_all x1, starting transfers between devices, local(): lax.all_to_all(jnp.stack((result, grad_rows)).reshape(2, n_expert, capaci...  4.14 us
    all_to_all x1, starting transfers between devices, local(): lax.all_to_all(parcel, 'expert', split_axis=1, concat_axis=1, tiled=True)  4.1 us
    dot_general x1, matrix products, expert_local(): jnp.dot(hidden, down_w, preferred_element_type=jnp.float32)  3.3 us
    dynamic_slice x2, local copies, waits for them, and re-layouts, other_sums(): piece = lax.dynamic_slice_in_dim(total, to * width, width, axis=1)  3.22 us
  transfers between devices with their start and end apart: 6, of which 4 were waited for; matrix products, arithmetic and copies ran while one was open for 26% of the time, Pallas kernels for 0%

profile of v1, /device:TPU:0, one launch (start us, length us, event | category | flops | bytes accessed | tf_op | source)
XLA Modules:
  0.0 99.7 jit_solution(14145739943017148776)
XLA Ops:
  0.6 0.0 copy-start
  0.6 5.1 %collective-permute-start.1 = (bf16[128,1792]{1,0:T(8,128)(2,1)}, bf16[128,1792]{1,0:T(8,128)(2,1)}, u32[]{:S(2)}, u32[]{:S(2)}) collective-permute-start(bf16[128,1792]{1,0:T(8,128)(2,1)} %bitcast.127), channel_id=1, source_target_pairs={{8,0},{16,8},{24,16},{0,24},{9,1},{17,9},{25,17},{1,25},{10,2},{18... | collective-permute-start | bytes 1376264 | tf_op jit(solution)/shard_map/ppermute | solution.py:10
  5.8 0.0 collective-permute-start
  5.8 0.8 slice_bitcast_fusion.1
  6.6 0.2 select_reduce_fusion
  6.8 2.7 %all-gather = bf16[1,128,3584]{2,1,0:T(8,128)(2,1)S(1)} all-gather(bf16[1,128,1792]{2,1,0:T(8,128)(2,1)} %param.15), channel_id=2, replica_groups=mesh['pipe'=4,'expert'=4,'tensor'=2] {'tensor'}, dimensions={2}, use_global_device_ids=true | all-gather | bytes 1376256 | tf_op jit(solution)/shard_map/all_gather | solution.py:129
  9.5 0.0 copy-start.2
  9.6 0.2 convolution_convert_fusion.1
  9.8 2.7 %fusion.13 = f32[128,512]{1,0:T(8,128)S(1)} fusion(bf16[1,3584,512]{2,1,0:T(8,128)(2,1)} %param.23, bf16[1,128,3584]{2,1,0:T(8,128)(2,1)S(1)} %all-gather), kind=kOutput, calls=%fused_computation.20 | convolution fusion | flops 469762048 | bytes 4849664 | tf_op jit(solution)/shard_map/dot_general | solution.py:89
  12.5 0.0 copy-done.2
  12.5 4.5 %collective-permute-done.1 = bf16[128,1792]{1,0:T(8,128)(2,1)} collective-permute-done((bf16[128,1792]{1,0:T(8,128)(2,1)}, bf16[128,1792]{1,0:T(8,128)(2,1)}, u32[]{:S(2)}, u32[]{:S(2)}) %collective-permute-start.1) | collective-permute-done | bytes 458784 | tf_op jit(solution)/shard_map/ppermute | solution.py:10
  17.0 2.7 %all_gather.11 = bf16[128,3584]{1,0:T(8,128)(2,1)S(1)} all-gather(bf16[128,1792]{1,0:T(8,128)(2,1)} %collective-permute-done.1), channel_id=1, replica_groups=mesh['pipe'=4,'expert'=4,'tensor'=2] {'tensor'}, dimensions={1}, use_global_device_ids=true | all-gather | bytes 1376256 | tf_op jit(solution)/shard_map/all_gather | solution.py:131
  19.7 0.0 copy-start.3
  19.7 0.9 fusion.2
  20.6 1.5 %stack.23 = bf16[1,2,1,4,3584]{4,3,1,2,0:T(4,128)(2,1)} reshape(bf16[8,3584]{1,0:T(8,128)(2,1)} %fusion.2) | data formatting | bytes 114688 | tf_op jit(solution)/shard_map/stack | solution.py:134
  22.0 0.0 copy-done.3
  22.1 4.4 %collective-permute-done = bf16[128,1792]{1,0:T(8,128)(2,1)S(1)} collective-permute-done((bf16[128,1792]{1,0:T(8,128)(2,1)}, bf16[128,1792]{1,0:T(8,128)(2,1)S(1)}, u32[]{:S(2)}, u32[]{:S(2)}) %collective-permute-start) | collective-permute-done | bytes 458784 | tf_op jit(solution)/shard_map/ppermute | solution.py:10
  26.5 2.5 %all_gather.9 = bf16[128,3584]{1,0:T(8,128)(2,1)S(1)} all-gather(bf16[128,1792]{1,0:T(8,128)(2,1)S(1)} %collective-permute-done), channel_id=1, replica_groups=mesh['pipe'=4,'expert'=4,'tensor'=2] {'tensor'}, dimensions={1}, use_global_device_ids=true | all-gather | bytes 1376256 | tf_op jit(solution)/shard_map/all_gather | solution.py:130
  29.0 0.2 convolution_convert_fusion.2
  29.2 1.0 maximum_bitcast_fusion
  30.2 0.1 copy.26
  30.2 0.8 broadcast_in_dim.69
  31.1 4.1 %all-to-all-start = ((bf16[3,4,4,3584]{3,2,0,1:T(4,128)(2,1)}), bf16[3,4,4,3584]{3,2,0,1:T(4,128)(2,1)}, u32[]{:S(2)}, u32[]{:S(2)}) async-start(bf16[3,4,4,3584]{3,2,0,1:T(4,128)(2,1)} %bitcast.11), calls=%async_computation | async-start | bytes 688128 | tf_op jit(solution)/shard_map/all_to_all | solution.py:143
  35.2 3.6 %fusion.3 = f32[128,512]{1,0:T(8,128)S(1)} fusion(bf16[128,3584]{1,0:T(8,128)(2,1)} %copy-done.3, bf16[1,512,3584]{2,1,0:T(8,128)(2,1)} %param.25), kind=kOutput, calls=%fused_computation.10 | convolution fusion | flops 469762048 | bytes 4849664 | tf_op jit(solution)/shard_map/dot_general | solution.py:23
  38.8 6.6 %fusion.11 = f32[128,3584]{1,0:T(8,128)} fusion(bf16[1,3584,512]{2,1,0:T(8,128)(2,1)} %param.23, f32[128,512]{1,0:T(8,128)S(1)} %fusion.3, bf16[1,3584,512]{2,1,0:T(8,128)(2,1)} %param.24, bf16[1,128,3584]{2,1,0:T(8,128)(2,1)} %copy-done.2, f32[128,512]{1,0:T(8,128)S(1)} %fusion.13), kind=kOutput, calls=%fused_computation.18 | convolution fusion | flops 940179456 | bytes 10616832 | tf_op jit(solution)/shard_map/dot_general | solution.py:23
  45.4 0.0 all-to-all-done
  45.4 1.8 %fusion.112 = (bf16[1,4,4,3584]{3,2,0,1:T(4,128)(2,1)}, bf16[1,4,4,3584]{3,2,0,1:T(4,128)(2,1)S(1)}, bf16[1,4,4,3584]{3,2,0,1:T(4,128)(2,1)S(1)}) fusion(bf16[3,4,4,3584]{3,2,0,1:T(4,128)(2,1)} %all-to-all-done), kind=kLoop, calls=%fused_computation.123 | loop fusion | bytes 688128 | tf_op jit(solution)/shard_map/slice | solution.py:145
  47.1 0.7 squeeze.56
  47.8 0.0 copy-start.1
  47.9 2.2 %fusion.17 = f32[16,256]{1,0:T(8,128)S(1)} fusion(bf16[16,3584]{1,0:T(8,128)(2,1)} %squeeze.56, bf16[1,1,256,3584]{3,2,1,0:T(8,128)(2,1)} %param.22), kind=kOutput, calls=%fused_computation.24 | convolution fusion | flops 29360128 | bytes 1966080 | tf_op jit(solution)/shard_map/dot_general | solution.py:23
  50.1 0.0 copy-done.1
  50.1 0.4 fusion.27
  50.5 0.0 copy-done
  50.5 3.5 %fusion.25 = f32[16,3584]{1,0:T(8,128)} fusion(bf16[1,1,3584,256]{3,2,1,0:T(8,128)(2,1)} %param.20, f32[16,256]{1,0:T(8,128)S(1)} %fusion.17, bf16[16,3584]{1,0:T(8,128)(2,1)S(1)} %squeeze.57, bf16[1,1,3584,256]{3,2,1,0:T(8,128)(2,1)S(1)} %copy-done, f32[16,256]{1,0:T(8,128)S(1)} %fusion.27), kind=kOutput, calls=%fused_computation.32 | convolution fusion | flops 58761216 | bytes 4046848 | tf_op jit(solution)/shard_map/dot_general | solution.py:23
  54.0 1.5 %fusion.1 = bf16[16,3584]{1,0:T(8,128)(2,1)S(1)} fusion(f32[16,3584]{1,0:T(8,128)} %fusion.25, bf16[1,1,3584,256]{3,2,1,0:T(8,128)(2,1)S(1)} %copy-done, f32[16,256]{1,0:T(8,128)S(1)} %fusion.17, f32[16,256]{1,0:T(8,128)S(1)} %fusion.27), kind=kOutput, calls=%fused_computation.4 | convolution fusion | flops 29499392 | bytes 2211840 | tf_op jit(solution)/shard_map/dot_general | solution.py:23
  55.5 0.9 squeeze.52
  56.5 1.8 %fusion.29 = f32[16,256]{1,0:T(8,128)S(1)} fusion(bf16[16,3584]{1,0:T(8,128)(2,1)S(1)} %squeeze.52, bf16[1,1,3584,256]{3,2,1,0:T(8,128)(2,1)} %param.20), kind=kOutput, calls=%fused_computation.36 | convolution fusion | flops 29360128 | bytes 1966080 | tf_op jit(solution)/shard_map/dot_general | solution.py:69
  58.3 3.3 %convolution_convert_fusion = bf16[16,3584]{1,0:T(8,128)(2,1)} fusion(bf16[1,1,256,3584]{3,2,1,0:T(8,128)(2,1)} %param.22, bf16[16,3584]{1,0:T(8,128)(2,1)S(1)} %squeeze.52, bf16[1,1,3584,256]{3,2,1,0:T(8,128)(2,1)S(1)} %copy-done, f32[16,256]{1,0:T(8,128)S(1)} %fusion.29), kind=kOutput, calls=%fused_computation.5 | convolution fusion | flops 58802176 | bytes 3915776 | tf_op jit(solution)/shard_map/dot_general | solution.py:72
  61.6 0.9 stack.25
  62.5 0.8 pad_maximum_fusion
  63.4 4.1 %all-to-all-start.1 = ((bf16[2,4,4,3584]{3,2,0,1:T(4,128)(2,1)}), bf16[2,4,4,3584]{3,2,0,1:T(4,128)(2,1)}, u32[]{:S(2)}, u32[]{:S(2)}) async-start(bf16[2,4,4,3584]{3,2,0,1:T(4,128)(2,1)} %pad_maximum_fusion), calls=%async_computation.1 | async-start | bytes 458752 | tf_op jit(solution)/shard_map/all_to_all | solution.py:146
  67.5 2.7 %fusion.9 = f32[128,512]{1,0:T(8,128)S(1)} fusion(bf16[128,3584]{1,0:T(8,128)(2,1)S(1)} %all_gather.9, bf16[1,3584,512]{2,1,0:T(8,128)(2,1)} %param.24), kind=kOutput, calls=%fused_computation.16 | convolution fusion | flops 469762048 | bytes 4849664 | tf_op jit(solution)/shard_map/dot_general | solution.py:86
  70.2 3.0 %all-to-all-done.1 = bf16[2,4,4,3584]{3,2,0,1:T(4,128)(2,1)} async-done(((bf16[2,4,4,3584]{3,2,0,1:T(4,128)(2,1)}), bf16[2,4,4,3584]{3,2,0,1:T(4,128)(2,1)}, u32[]{:S(2)}, u32[]{:S(2)}) %all-to-all-start.1) | async-done | bytes 229408 | tf_op jit(solution)/shard_map/all_to_all | solution.py:146
  73.2 1.7 %fusion.113 = (bf16[1,4,4,3584]{3,2,0,1:T(4,128)(2,1)}, bf16[1,4,4,3584]{3,2,0,1:T(4,128)(2,1)}) fusion(bf16[2,4,4,3584]{3,2,0,1:T(4,128)(2,1)} %all-to-all-done.1), kind=kLoop, calls=%fused_computation.124 | loop fusion | bytes 458752 | tf_op jit(solution)/shard_map/slice | solution.py:160
  74.9 1.6 %squeeze.58 = bf16[16,3584]{1,0:T(8,128)(2,1)} reshape(bf16[1,4,4,3584]{3,2,0,1:T(4,128)(2,1)} %get-tuple-element.10) | data formatting | bytes 229376 | tf_op jit(solution)/shard_map/squeeze | solution.py:159
  76.5 2.6 %fusion.71 = f32[128,3584]{1,0:T(8,128)} fusion(bf16[16,3584]{1,0:T(8,128)(2,1)} %squeeze.58, bf16[16,128]{1,0:T(8,128)(2,1)S(1)} %bitcast.123, bf16[16,128]{1,0:T(8,128)(2,1)S(1)} %bitcast.124), kind=kOutput, calls=%fused_computation.61 | convolution fusion | flops 29835264 | bytes 1957888 | tf_op jit(solution)/shard_map/dot_general | solution.py:52
  79.1 6.2 %convolution_add_fusion.1 = f32[128,3584]{1,0:T(8,128)} fusion(f32[128,3584]{1,0:T(8,128)} %fusion.71, bf16[1,512,3584]{2,1,0:T(8,128)(2,1)} %param.25, f32[128,512]{1,0:T(8,128)S(1)} %fusion.9, bf16[128,3584]{1,0:T(8,128)(2,1)S(1)} %all_gather.9, bf16[1,3584,512]{2,1,0:T(8,128)(2,1)} %param.23), kind=kOutput, calls=%fused_computation.2 | convolution fusion | flops 940376064 | bytes 12189696 | tf_op jit(solution)/shard_map/dot_general | solution.py:88
  85.3 0.0 copy-start.7
  85.3 2.2 %constant_dynamic-slice_fusion = f32[128,1792]{1,0:T(8,128)} fusion(f32[128,3584]{1,0:T(8,128)} %convolution_add_fusion.1, s32[]{:T(128)S(6)} %select_n.74), kind=kLoop, calls=%fused_computation.113 | loop fusion | bytes 1835012 | tf_op jit(solution)/shard_map/dynamic_slice | solution.py:63
  87.5 0.0 collective-permute-start.2
  87.5 0.0 copy-done.7
  87.6 0.0 copy-start.6
  87.6 0.4 fusion.114
  88.0 1.1 %copy-done.6 = f32[128,3584]{1,0:T(8,128)S(1)} copy-done((f32[128,3584]{1,0:T(8,128)S(1)}, f32[128,3584]{1,0:T(8,128)}, u32[]{:S(2)}) %copy-start.6) | copy-done | bytes 1835032
  89.1 3.4 %fusion = f32[128,3584]{1,0:T(8,128)S(1)} fusion(f32[128,3584]{1,0:T(8,128)S(1)} %fusion.114, f32[128,3584]{1,0:T(8,128)S(1)} %copy-done.6, bf16[1,3584,512]{2,1,0:T(8,128)(2,1)} %param.24, f32[128,512]{1,0:T(8,128)S(1)} %fusion.3, f32[128,512]{1,0:T(8,128)S(1)} %fusion.13), kind=kOutput, calls=%fused_computation.1 | convolution fusion | flops 471072768 | bytes 9699328 | tf_op jit(solution)/shard_map/dot_general | solution.py:23
  92.4 0.0 copy-start.4
  92.5 1.3 %copy-done.4 = f32[128,3584]{1,0:T(8,128)} copy-done((f32[128,3584]{1,0:T(8,128)}, f32[128,3584]{1,0:T(8,128)S(1)}, u32[]{:S(2)}) %copy-start.4) | copy-done | bytes 1835032
  93.7 1.0 %constant_dynamic-slice_fusion.1 = f32[128,1792]{1,0:T(8,128)} fusion(f32[128,3584]{1,0:T(8,128)S(1)} %fusion, s32[]{:T(128)S(6)} %select_n.74), kind=kLoop, calls=%fused_computation.114 | loop fusion | bytes 1835012 | tf_op jit(solution)/shard_map/dynamic_slice | solution.py:63
  94.7 0.5 collective-permute-start.3
  95.2 0.0 collective-permute-done.2
  95.2 2.2 %fusion.65 = bf16[1,128,1792]{2,1,0:T(8,128)(2,1)} fusion(f32[128,1792]{1,0:T(8,128)S(1)} %collective-permute-done.2, f32[128,3584]{1,0:T(8,128)} %convolution_add_fusion.1, s32[]{:T(128)S(6)} %select_n.72), kind=kLoop, calls=%fused_computation.51 | loop fusion | flops 458752 | bytes 2293764 | tf_op jit(solution)/shard_map/broadcast_in_dim | solution.py:166
  97.4 0.3 collective-permute-done.3
  97.7 0.0 copy-done.5
  97.7 2.0 %fusion.66 = bf16[1,128,1792]{2,1,0:T(8,128)(2,1)} fusion(f32[128,1792]{1,0:T(8,128)} %collective-permute-done.3, f32[128,3584]{1,0:T(8,128)S(1)} %copy-done.5, s32[]{:T(128)S(6)} %select_n.72), kind=kLoop, calls=%fused_computation.52 | loop fusion | flops 458752 | bytes 2293764 | tf_op jit(solution)/shard_map/broadcast_in_dim | solution.py:166
  (13 shorter events, 0.2 us)
Async XLA Ops:
  0.6 49.9 %copy-start = (bf16[1,1,3584,256]{3,2,1,0:T(8,128)(2,1)S(1)}, bf16[1,1,3584,256]{3,2,1,0:T(8,128)(2,1)}, u32[]{:S(2)}) copy-start(bf16[1,1,3584,256]{3,2,1,0:T(8,128)(2,1)} %param.21) | copy-start | bytes 5505028
  0.6 16.4 %collective-permute-start.1 = (bf16[128,1792]{1,0:T(8,128)(2,1)}, bf16[128,1792]{1,0:T(8,128)(2,1)}, u32[]{:S(2)}, u32[]{:S(2)}) collective-permute-start(bf16[128,1792]{1,0:T(8,128)(2,1)} %bitcast.127), channel_id=1, source_target_pairs={{8,0},{16,8},{24,16},{0,24},{9,1},{17,9},{25,17},{1,25},{10,2},{18... | collective-permute-start | bytes 1376264 | tf_op jit(solution)/shard_map/ppermute | solution.py:10
  5.8 20.7 %collective-permute-start = (bf16[128,1792]{1,0:T(8,128)(2,1)}, bf16[128,1792]{1,0:T(8,128)(2,1)S(1)}, u32[]{:S(2)}, u32[]{:S(2)}) collective-permute-start(bf16[128,1792]{1,0:T(8,128)(2,1)} %bitcast.128), channel_id=1, source_target_pairs={{24,0},{0,8},{8,16},{16,24},{25,1},{1,9},{9,17},{17,25},{26,2},{2,... | collective-permute-start | bytes 1376264 | tf_op jit(solution)/shard_map/ppermute | solution.py:10
  9.5 3.0 %copy-start.2 = (bf16[1,128,3584]{2,1,0:T(8,128)(2,1)}, bf16[1,128,3584]{2,1,0:T(8,128)(2,1)S(1)}, u32[]{:S(2)}) copy-start(bf16[1,128,3584]{2,1,0:T(8,128)(2,1)S(1)} %all-gather) | copy-start | bytes 2752516
  19.7 2.4 %copy-start.3 = (bf16[128,3584]{1,0:T(8,128)(2,1)}, bf16[128,3584]{1,0:T(8,128)(2,1)S(1)}, u32[]{:S(2)}) copy-start(bf16[128,3584]{1,0:T(8,128)(2,1)S(1)} %all_gather.11) | copy-start | bytes 2752516
  31.1 14.3 %all-to-all-start = ((bf16[3,4,4,3584]{3,2,0,1:T(4,128)(2,1)}), bf16[3,4,4,3584]{3,2,0,1:T(4,128)(2,1)}, u32[]{:S(2)}, u32[]{:S(2)}) async-start(bf16[3,4,4,3584]{3,2,0,1:T(4,128)(2,1)} %bitcast.11), calls=%async_computation | async-start | bytes 688128 | tf_op jit(solution)/shard_map/all_to_all | solution.py:143
  47.8 2.3 %copy-start.1 = (bf16[1,1,3584,256]{3,2,1,0:T(8,128)(2,1)S(1)}, bf16[1,1,3584,256]{3,2,1,0:T(8,128)(2,1)}, u32[]{:S(2)}) copy-start(bf16[1,1,3584,256]{3,2,1,0:T(8,128)(2,1)} %param.20) | copy-start | bytes 5505028
  63.4 9.8 %all-to-all-start.1 = ((bf16[2,4,4,3584]{3,2,0,1:T(4,128)(2,1)}), bf16[2,4,4,3584]{3,2,0,1:T(4,128)(2,1)}, u32[]{:S(2)}, u32[]{:S(2)}) async-start(bf16[2,4,4,3584]{3,2,0,1:T(4,128)(2,1)} %pad_maximum_fusion), calls=%async_computation.1 | async-start | bytes 458752 | tf_op jit(solution)/shard_map/all_to_all | solution.py:146
  85.3 2.2 %copy-start.7 = (bf16[1,4,4,3584]{3,2,0,1:T(4,128)(2,1)S(1)}, bf16[1,4,4,3584]{3,2,0,1:T(4,128)(2,1)}, u32[]{:S(2)}) copy-start(bf16[1,4,4,3584]{3,2,0,1:T(4,128)(2,1)} %get-tuple-element.9) | copy-start | bytes 344068
  87.5 7.7 %collective-permute-start.2 = (f32[128,1792]{1,0:T(8,128)}, f32[128,1792]{1,0:T(8,128)S(1)}, u32[]{:S(2)}, u32[]{:S(2)}) collective-permute-start(f32[128,1792]{1,0:T(8,128)} %constant_dynamic-slice_fusion), channel_id=1, source_target_pairs={{1,0},{0,1},{3,2},{2,3},{5,4},{4,5},{7,6},{6,7},{9,8},{8,9},{11,10... | collective-permute-start | bytes 2752520 | tf_op jit(solution)/shard_map/ppermute | solution.py:10
  87.6 1.5 %copy-start.6 = (f32[128,3584]{1,0:T(8,128)S(1)}, f32[128,3584]{1,0:T(8,128)}, u32[]{:S(2)}) copy-start(f32[128,3584]{1,0:T(8,128)} %fusion.11) | copy-start | bytes 5505028
  92.4 1.3 %copy-start.4 = (f32[128,3584]{1,0:T(8,128)}, f32[128,3584]{1,0:T(8,128)S(1)}, u32[]{:S(2)}) copy-start(f32[128,3584]{1,0:T(8,128)S(1)} %fusion) | copy-start | bytes 5505028
  94.7 2.9 %collective-permute-start.3 = (f32[128,1792]{1,0:T(8,128)}, f32[128,1792]{1,0:T(8,128)}, u32[]{:S(2)}, u32[]{:S(2)}) collective-permute-start(f32[128,1792]{1,0:T(8,128)} %constant_dynamic-slice_fusion.1), channel_id=1, source_target_pairs={{1,0},{0,1},{3,2},{2,3},{5,4},{4,5},{7,6},{6,7},{9,8},{8,9},{11,10... | collective-permute-start | bytes 2752520 | tf_op jit(solution)/shard_map/ppermute | solution.py:10
  95.2 2.4 %copy-start.5 = (f32[128,3584]{1,0:T(8,128)S(1)}, f32[128,3584]{1,0:T(8,128)}, u32[]{:S(2)}) copy-start(f32[128,3584]{1,0:T(8,128)} %copy-done.4) | copy-start | bytes 5505028

commit v2 on v1

v2 whole, which is shorter than its diff:
```python
import functools

import jax
import jax.numpy as jnp
from jax import lax
from jax.experimental import pallas as pl
from jax.experimental.pallas import tpu as pltpu
from jax.sharding import PartitionSpec as P

MESH = pl.DeviceIdType.MESH
ROW_CHUNKS = 4
F32 = jnp.float32
BF16 = jnp.bfloat16


def swish(values):
    return values * jax.nn.sigmoid(values)


def swish_slope(values):
    logistic = jax.nn.sigmoid(values)
    return logistic * (1.0 + values * (1.0 - logistic))


def dot(left, right):
    return jnp.dot(left, right, preferred_element_type=F32)


def contract_last(left, right):
    return lax.dot_general(left, right, (((1,), (1,)), ((), ())), preferred_element_type=F32)


def chunk_of(width):
    return 256 if width % 256 == 0 else 128


def kernel(
    sizes,
    x_prev, c_next, saved, ids, keep, slot, level,
    gate_r_hbm, up_r_hbm, down_r_hbm, gate_s_hbm, up_s_hbm, down_s_hbm,
    out_ref, grad_ref,
    gate_r, up_r, down_r, gate_s, up_s, down_s,
    full_x, full_c, full_s,
    a_saved, b_saved, hidden, grad_gate, grad_up,
    a_routed, b_routed,
    send_early, send_late, recv_early, recv_late, rows_early, rows_late,
    ret_send, ret_recv, ret_rows,
    part_out, part_grad, peer_out, peer_grad,
    weight_sem, saved_sem, saved_send, saved_recv,
    pipe_send, pipe_recv, fwd_send, fwd_recv,
    early_send, early_recv, late_send, late_recv, self_sem,
    ret_ssem, ret_rsem, part_send, part_recv,
):
    n_pipe, ne, nt, capacity = sizes
    tokens, width = x_prev.shape
    features = width * nt
    experts = ne // 2
    group = 2 * capacity
    me_p, me_e, me_t = lax.axis_index("pipe"), lax.axis_index("expert"), lax.axis_index("tensor")
    nxt, prv = lax.rem(me_p + 1, n_pipe), lax.rem(me_p + n_pipe - 1, n_pipe)
    my_cols = pl.ds(pl.multiple_of(me_t * width, 128), width)

    def peer_t(step):
        return lax.rem(me_t + step, nt)

    def peer_e(step):
        return lax.rem(me_e + step, ne)

    def remote(src, dst, ssem, rsem, device):
        return pltpu.make_async_remote_copy(
            src_ref=src, dst_ref=dst, send_sem=ssem, recv_sem=rsem,
            device_id=device, device_id_type=MESH,
        )

    saved_local = pltpu.make_async_copy(saved, full_s.at[:, my_cols], saved_sem)
    saved_local.start()
    loads = {}
    pairs = (
        (gate_s_hbm, gate_s), (up_s_hbm, up_s), (gate_r_hbm, gate_r),
        (up_r_hbm, up_r), (down_s_hbm, down_s), (down_r_hbm, down_r),
    )
    for n, (src, dst) in enumerate(pairs):
        loads[n] = pltpu.make_async_copy(src, dst, weight_sem.at[n])
        loads[n].start()

    barrier = pltpu.get_barrier_semaphore()
    greeted = [{"pipe": nxt}, {"pipe": prv}]
    for se in range(ne):
        for st in range(nt):
            if se or st:
                greeted.append({"expert": peer_e(se), "tensor": peer_t(st)})
    for device in greeted:
        pl.semaphore_signal(barrier, inc=1, device_id=device, device_id_type=MESH)
    pl.semaphore_wait(barrier, len(greeted))

    step_rows = tokens // ROW_CHUNKS
    pipe_copies = []
    for q in range(ROW_CHUNKS):
        rows = pl.ds(q * step_rows, step_rows)
        for a, (src, dst, to) in enumerate(((x_prev, full_x, nxt), (c_next, full_c, prv))):
            copy = remote(
                src.at[rows, :], dst.at[rows, my_cols],
                pipe_send.at[a, q], pipe_recv.at[a, q], {"pipe": to},
            )
            copy.start()
            pipe_copies.append(copy)
    saved_copies = []
    for st in range(1, nt):
        copy = remote(
            saved, full_s.at[:, my_cols], saved_send.at[st - 1], saved_recv.at[st - 1],
            {"tensor": peer_t(st)},
        )
        copy.start()
        saved_copies.append(copy)

    def targets(m):
        return jnp.where(keep[m] > 0, ids[m] * capacity + slot[m], -1)

    target_f, target_b = targets(0), targets(1)

    def table(target, values, slots_at):
        total = jnp.zeros((tokens, slots_at.shape[1]), jnp.int32)
        for k in range(target.shape[1]):
            total = total + jnp.where(target[:, k:k + 1] == slots_at, values[:, k:k + 1], 0)
        return total

    lanes = ((experts * group + 127) // 128) * 128
    place = lax.broadcasted_iota(jnp.int32, (tokens, lanes), 1)
    inside = lax.rem(place, group)
    owner = lax.div(place, group)
    slots_x = jnp.where(inside < capacity, owner * capacity + inside, -2)
    slots_c = jnp.where(inside >= capacity, owner * capacity + inside - capacity, -2)
    ones = jnp.ones(target_f.shape, jnp.int32)
    used = experts * group
    pick_x = table(target_f, ones, slots_x).astype(F32).T[:used].astype(BF16)
    pick_c = table(target_b, ones, slots_c).astype(F32).T[:used].astype(BF16)
    scale_c = jnp.sum(
        table(target_b, level[1], slots_c).astype(F32).T[:used], axis=1, keepdims=True
    ) / 4096.0

    parts = ne * nt * group
    lanes = ((parts + 127) // 128) * 128
    place = lax.broadcasted_iota(jnp.int32, (tokens, lanes), 1)
    inside = lax.rem(place, group)
    owner = lax.div(place, 2 * nt * group)
    slots_o = jnp.where(inside < capacity, owner * capacity + inside, -2)
    slots_g = jnp.where(inside >= capacity, owner * capacity + inside - capacity, -2)
    level_o = table(target_f, level[0], slots_o)
    high = lax.div(level_o, 64)
    low = level_o - high * 64
    factor_high = (high.astype(F32) / 64.0).astype(BF16)[:, :parts]
    factor_low = (low.astype(F32) / 4096.0).astype(BF16)[:, :parts]
    factor_grad = table(target_b, ones, slots_g).astype(F32).astype(BF16)[:, :parts]

    saved_local.wait()
    for copy in saved_copies:
        copy.wait_recv()
    cf = chunk_of(features)

    def exchange(buffer, landing, ssem, rsem, self_index):
        copies = []
        for se in range(1, ne):
            to = peer_e(se)
            copy = remote(
                buffer.at[lax.div(to, 2)], landing.at[me_e], ssem.at[se - 1], rsem.at[se - 1],
                {"expert": to},
            )
            copy.start()
            copies.append(copy)
        own = pltpu.make_async_copy(
            buffer.at[lax.div(me_e, 2)], landing.at[me_e], self_sem.at[self_index]
        )
        own.start()
        return copies, own

    def early_rows(n, carry):
        cols = pl.ds(pl.multiple_of(n * cf, 128), cf)
        picked = dot(pick_c, full_s[:, cols])
        for e in range(experts):
            send_early[e, :, cols] = picked[e * group:(e + 1) * group].astype(BF16)
        return carry

    lax.fori_loop(0, features // cf, early_rows, 0)
    early_copies, early_own = exchange(send_early, recv_early, early_send, early_recv, 0)

    def gather_rows(landing, dest):
        for i in range(0, ne, 2):
            both = jnp.concatenate(
                (landing[i].astype(F32), landing[i + 1].astype(F32)), axis=0
            )
            dest[i * group:(i + 2) * group, :] = both.astype(BF16)

    loads[0].wait()
    loads[1].wait()
    cs = chunk_of(gate_s.shape[1])

    def shared_saved(n, carry):
        cols = pl.ds(pl.multiple_of(n * cs, 128), cs)
        a_saved[:, cols] = dot(full_s[...], gate_s[:, cols])
        b_saved[:, cols] = dot(full_s[...], up_s[:, cols])
        return carry

    lax.fori_loop(0, gate_s.shape[1] // cs, shared_saved, 0)

    fwd_copies = []

    def forward(q):
        rows = pl.ds(q * step_rows, step_rows)
        for a, held in enumerate((full_x, full_c)):
            pipe_copies[2 * q + a].wait_recv()
            for st in range(1, nt):
                copy = remote(
                    held.at[rows, my_cols], held.at[rows, my_cols],
                    fwd_send.at[a, q, st - 1], fwd_recv.at[a, q, st - 1], {"tensor": peer_t(st)},
                )
                copy.start()
                fwd_copies.append(copy)

    for q in range(ROW_CHUNKS // 2):
        forward(q)

    for copy in early_copies:
        copy.wait_recv()
    early_own.wait()
    gather_rows(recv_early, rows_early)
    loads[2].wait()
    loads[3].wait()
    a_routed[...] = dot(rows_early[...], gate_r[...])
    b_routed[...] = dot(rows_early[...], up_r[...])

    for q in range(ROW_CHUNKS // 2, ROW_CHUNKS):
        forward(q)
    for copy in fwd_copies:
        copy.wait_recv()

    def late_rows(n, carry):
        cols = pl.ds(pl.multiple_of(n * cf, 128), cf)
        picked = dot(pick_x, full_x[:, cols]) + scale_c * dot(pick_c, full_c[:, cols])
        for e in range(experts):
            send_late[e, :, cols] = picked[e * group:(e + 1) * group].astype(BF16)
        return carry

    lax.fori_loop(0, features // cf, late_rows, 0)
    late_copies, late_own = exchange(send_late, recv_late, late_send, late_recv, 1)

    loads[4].wait()

    def shared_first(n, carry):
        cols = pl.ds(pl.multiple_of(n * cs, 128), cs)
        gate_pre = dot(full_x[...], gate_s[:, cols])
        up_pre = dot(full_x[...], up_s[:, cols])
        hidden[:, cols] = (swish(gate_pre) * up_pre).astype(BF16)
        grad_hidden = contract_last(full_c[...], down_s[cols, :])
        gate_back = a_saved[:, cols]
        grad_gate[:, cols] = (grad_hidden * b_saved[:, cols] * swish_slope(gate_back)).astype(BF16)
        grad_up[:, cols] = (grad_hidden * swish(gate_back)).astype(BF16)
        return carry

    lax.fori_loop(0, gate_s.shape[1] // cs, shared_first, 0)

    loads[5].wait()
    for copy in late_copies:
        copy.wait_recv()
    late_own.wait()
    gather_rows(recv_late, rows_late)
    gate_pre = dot(rows_late[...], gate_r[...])
    up_pre = dot(rows_late[...], up_r[...])
    grad_hidden = contract_last(rows_late[...], down_r[...])
    gate_back = a_routed[...]
    row = lax.broadcasted_iota(jnp.int32, gate_pre.shape, 0)
    ahead = lax.rem(row, group) < capacity
    hidden_r = jnp.where(ahead, swish(gate_pre) * up_pre, 0.0).astype(BF16)
    gate_grad_r = jnp.where(
        ahead, 0.0, grad_hidden * b_routed[...] * swish_slope(gate_back)
    ).astype(BF16)
    up_grad_r = jnp.where(ahead, 0.0, grad_hidden * swish(gate_back)).astype(BF16)
    cw = chunk_of(width)
    for c in range(nt):
        def routed_second(n, carry, c=c):
            at = pl.ds(pl.multiple_of(n * cw, 128), cw)
            cols = pl.ds(pl.multiple_of(c * width + n * cw, 128), cw)
            total = (
                dot(hidden_r, down_r[:, cols])
                + contract_last(gate_grad_r, gate_r[cols, :])
                + contract_last(up_grad_r, up_r[cols, :])
            )
            for i in range(ne):
                ret_send[i, c, :, at] = total[i * group:(i + 1) * group].astype(BF16)
            return carry

        lax.fori_loop(0, width // cw, routed_second, 0)

    ret_copies = []
    for se in range(ne):
        for st in range(nt):
            if se or st:
                to_e, to_t = peer_e(se), peer_t(st)
                n = se * nt + st - 1
                copy = remote(
                    ret_send.at[to_e, to_t], ret_recv.at[me_e, me_t],
                    ret_ssem.at[n], ret_rsem.at[n], {"expert": to_e, "tensor": to_t},
                )
                copy.start()
                ret_copies.append(copy)
    ret_own = pltpu.make_async_copy(
        ret_send.at[me_e, me_t], ret_recv.at[me_e, me_t], self_sem.at[2]
    )
    ret_own.start()

    part_copies = []
    for st in list(range(1, nt)) + [0]:
        to = peer_t(st)

        def shared_second(n, carry, st=st, to=to):
            at = pl.ds(pl.multiple_of(n * cw, 128), cw)
            cols = pl.ds(pl.multiple_of(to * width + n * cw, 128), cw)
            part_out[st, :, at] = dot(hidden[...], down_s[:, cols])
            part_grad[st, :, at] = contract_last(grad_gate[...], gate_s[cols, :]) + contract_last(
                grad_up[...], up_s[cols, :]
            )
            return carry

        lax.fori_loop(0, width // cw, shared_second, 0)
        if st:
            for a, (src, dst) in enumerate(((part_out, peer_out), (part_grad, peer_grad))):
                copy = remote(
                    src.at[st], dst.at[st - 1], part_send.at[a, st - 1], part_recv.at[a, st - 1],
                    {"tensor": to},
                )
                copy.start()
                part_copies.append(copy)

    for copy in ret_copies:
        copy.wait_recv()
    ret_own.wait()
    for i in range(0, ne * nt, 2):
        first, second = divmod(i, nt), divmod(i + 1, nt)
        both = jnp.concatenate((ret_recv[first].astype(F32), ret_recv[second].astype(F32)), axis=0)
        ret_rows[i * group:(i + 2) * group, :] = both.astype(BF16)
    for copy in part_copies:
        copy.wait_recv()

    def finish(n, carry):
        at = pl.ds(pl.multiple_of(n * cw, 128), cw)
        rows = ret_rows[:, at]
        out_sum = part_out[0, :, at] + (dot(factor_high, rows) + dot(factor_low, rows))
        grad_sum = part_grad[0, :, at] + dot(factor_grad, rows)
        for st in range(1, nt):
            out_sum = out_sum + peer_out[st - 1, :, at]
            grad_sum = grad_sum + peer_grad[st - 1, :, at]
        out_ref[:, at] = out_sum.astype(BF16)
        grad_ref[:, at] = grad_sum.astype(BF16)
        return carry

    lax.fori_loop(0, width // cw, finish, 0)

    for copy in (
        pipe_copies + saved_copies + fwd_copies + early_copies + late_copies + ret_copies
        + part_copies
    ):
        copy.wait_send()


def local(
    inputs_prev, cotangent_next, saved_input, expert_ids, keep_mask, slot_pos, weight_q,
    gate_routed, up_routed, down_routed, gate_shared, up_shared, down_shared,
):
    n_pipe, ne, nt = lax.axis_size("pipe"), lax.axis_size("expert"), lax.axis_size("tensor")
    tokens, width = inputs_prev.shape[1:]
    features = width * nt
    capacity = tokens // 32
    group = 2 * capacity
    experts = ne // 2
    fr, fs = gate_routed.shape[3], gate_shared.shape[2]
    vmem = pl.BlockSpec(memory_space=pltpu.VMEM)
    hbm = pl.BlockSpec(memory_space=pl.ANY)
    dma = pltpu.SemaphoreType.DMA
    shape = jax.ShapeDtypeStruct((tokens, width), BF16)
    out, grad = pl.pallas_call(
        functools.partial(kernel, (n_pipe, ne, nt, capacity)),
        out_shape=(shape, shape),
        in_specs=[hbm] * 3 + [vmem] * 4 + [hbm] * 6,
        out_specs=(vmem, vmem),
        scratch_shapes=[
            pltpu.VMEM((features, fr), BF16),
            pltpu.VMEM((features, fr), BF16),
            pltpu.VMEM((fr, features), BF16),
            pltpu.VMEM((features, fs), BF16),
            pltpu.VMEM((features, fs), BF16),
            pltpu.VMEM((fs, features), BF16),
            pltpu.VMEM((tokens, features), BF16),
            pltpu.VMEM((tokens, features), BF16),
            pltpu.VMEM((tokens, features), BF16),
            pltpu.VMEM((tokens, fs), F32),
            pltpu.VMEM((tokens, fs), F32),
            pltpu.VMEM((tokens, fs), BF16),
            pltpu.VMEM((tokens, fs), BF16),
            pltpu.VMEM((tokens, fs), BF16),
            pltpu.VMEM((ne * group, fr), F32),
            pltpu.VMEM((ne * group, fr), F32),
            pltpu.VMEM((experts, group, features), BF16),
            pltpu.VMEM((experts, group, features), BF16),
            pltpu.VMEM((ne, group, features), BF16),
            pltpu.VMEM((ne, group, features), BF16),
            pltpu.VMEM((ne * group, features), BF16),
            pltpu.VMEM((ne * group, features), BF16),
            pltpu.VMEM((ne, nt, group, width), BF16),
            pltpu.VMEM((ne, nt, group, width), BF16),
            pltpu.VMEM((ne * nt * group, width), BF16),
            pltpu.VMEM((nt, tokens, width), F32),
            pltpu.VMEM((nt, tokens, width), F32),
            pltpu.VMEM((nt - 1, tokens, width), F32),
            pltpu.VMEM((nt - 1, tokens, width), F32),
            dma((6,)),
            dma,
            dma((nt - 1,)),
            dma((nt - 1,)),
            dma((2, ROW_CHUNKS)),
            dma((2, ROW_CHUNKS)),
            dma((2, ROW_CHUNKS, nt - 1)),
            dma((2, ROW_CHUNKS, nt - 1)),
            dma((ne - 1,)),
            dma((ne - 1,)),
            dma((ne - 1,)),
            dma((ne - 1,)),
            dma((3,)),
            dma((ne * nt - 1,)),
            dma((ne * nt - 1,)),
            dma((2, nt - 1)),
            dma((2, nt - 1)),
        ],
        compiler_params=pltpu.CompilerParams(collective_id=0, has_side_effects=True),
        name="moe_step",
    )(
        inputs_prev[0], cotangent_next[0], saved_input[0],
        expert_ids[:, 0], keep_mask[:, 0], slot_pos[:, 0], weight_q[:, 0],
        gate_routed[0, 0], up_routed[0, 0], down_routed[0, 0],
        gate_shared[0], up_shared[0], down_shared[0],
    )
    return out[None], grad[None]


def solution(mesh):
    return jax.shard_map(
        local,
        mesh=mesh,
        in_specs=(
            P("pipe", "expert", "tensor"),
            P("pipe", "expert", "tensor"),
            P("pipe", "expert", "tensor"),
            P(None, "pipe", "expert", None),
            P(None, "pipe", "expert", None),
            P(None, "pipe", "expert", None),
            P(None, "pipe", "expert", None),
            P("pipe", "expert", None, "tensor"),
            P("pipe", "expert", None, "tensor"),
            P("pipe", "expert", "tensor", None),
            P("pipe", None, "tensor"),
            P("pipe", None, "tensor"),
            P("pipe", "tensor", None),
        ),
        out_specs=(P("pipe", "expert", "tensor"), P("pipe", "expert", "tensor")),
        check_vma=False,
    )
```

time: 101 us -> 58.1 us (0.58)
  Pallas kernels: 0 us -> 47.5 us
  matrix products: 42.3 us -> 0 us
  starting transfers between devices: 13.9 us -> 0 us
  waiting for transfers between devices: 12.2 us -> 0 us
  blocking collectives: 7.79 us -> 0 us
  other arithmetic: 7.08 us -> 0 us
  local copies, waits for them, and re-layouts: 15.7 us -> 9.57 us
    pallas_call x0 -> x1, Pallas kernels: none -> 47.5 us  [local(): pl.pallas_call(functools.partial(kernel, (n_pipe, ne, nt, capacity)), out...]
    dot_general x17 -> x0, matrix products: 42.3 us -> none  [the longest x6 20.8 us: contract_last(): lax.dot_general(left, right, (((1,), (1,)), ((), ())), preferred_element_...]
    ppermute x4 -> x0, waiting for transfers between devices: 9.2 us -> none  [passed_along(): return lax.ppermute(block, axis, route)]
    all_to_all x2 -> x0, starting transfers between devices: 8.25 us -> none  [the longest x1 4.14 us: local(): lax.all_to_all(jnp.stack((result, grad_rows)).reshape(2, n_expert, capaci...]
    all_gather x3 -> x0, blocking collectives: 7.79 us -> none  [the longest x1 2.67 us: local(): full_saved = lax.all_gather(saved_input[0], 'tensor', axis=1, tiled=True)]
    unnamed x16 -> x6, local copies, waits for them, and re-layouts: 2.35 us -> 9.57 us
    broadcast_in_dim x4 -> x0, other arithmetic: 5.96 us -> none  [the longest x1 2.16 us: local(): summed_out.astype(jnp.bfloat16)[None]]
    ppermute x4 -> x0, starting transfers between devices: 5.64 us -> none  [passed_along(): return lax.ppermute(block, axis, route)]
  transfers between devices with their start and end apart: 6 -> 0, of which waited for: 4 -> 0; matrix products, arithmetic and copies ran while one was open for 26% -> 0% of each run, Pallas kernels for 0% -> 0%
where the time goes in v2:
time: 58.1 us; the launch traced here: 57.7 us
  Pallas kernels  47.5 us (82%)
  local copies, waits for them, and re-layouts  9.57 us (16%)
  between operations  0.64 us (1%)
    pallas_call x1, Pallas kernels, local(): pl.pallas_call(functools.partial(kernel, (n_pipe, ne, nt, capacity)), out...  47.5 us
    unnamed x6, local copies, waits for them, and re-layouts  9.57 us

profile of v2, /device:TPU:0, one launch (start us, length us, event | category | flops | bytes accessed | tf_op | source)
XLA Modules:
  0.0 57.7 jit_solution(15670334446097042915)
XLA Ops:
  0.6 1.5 %copy.15 = s32[2,1,128,8]{3,2,0,1:T(8,128)} copy(s32[2,1,128,8]{2,3,1,0:T(8,128)} %param.16) | data formatting | bytes 16384 | tf_op args[3]
  2.1 1.5 %copy.16 = s32[2,1,128,8]{3,2,0,1:T(8,128)} copy(s32[2,1,128,8]{2,3,1,0:T(8,128)} %param.17) | data formatting | bytes 16384 | tf_op args[4]
  3.6 1.5 %copy.17 = s32[2,1,128,8]{3,2,0,1:T(8,128)} copy(s32[2,1,128,8]{2,3,1,0:T(8,128)} %param.18) | data formatting | bytes 16384 | tf_op args[5]
  5.1 1.5 %copy.18 = s32[2,1,128,8]{3,2,0,1:T(8,128)} copy(s32[2,1,128,8]{2,3,1,0:T(8,128)} %param.19) | data formatting | bytes 16384 | tf_op args[6]
  6.6 47.5 %moe_step.1 = (bf16[128,1792]{1,0:T(8,128)(2,1)}, bf16[128,1792]{1,0:T(8,128)(2,1)}) custom-call(bf16[128,1792]{1,0:T(8,128)(2,1)} %bitcast.27, bf16[128,1792]{1,0:T(8,128)(2,1)} %bitcast.28, bf16[128,1792]{1,0:T(8,128)(2,1)} %bitcast.29, s32[2,128,8]{2,1,0:T(8,128)} %bitcast.21, s32[2,128,8]{2,1,0:T(8,128)} %bitcast.22, s32[2,128,8]{2,1,0:T(8,128)} %bitcast.23, ...), custom_call_target="tpu_custom_call" | custom-call | tf_op jit(solution)/shard_map/moe_step/pallas_call | solution.py:379
  54.1 1.8 %copy.21 = bf16[1,128,1792]{2,1,0:T(8,128)(2,1)} copy(bf16[1,128,1792]{2,1,0:T(8,128)(2,1)} %bitcast.26) | data formatting | bytes 917504
  55.9 1.8 %copy.22 = bf16[1,128,1792]{2,1,0:T(8,128)(2,1)} copy(bf16[1,128,1792]{2,1,0:T(8,128)(2,1)} %bitcast.25) | data formatting | bytes 917504

commit v3 on v2

--- a/solution.py
+++ b/solution.py
@@ -119,28 +119,26 @@
     target_f, target_b = targets(0), targets(1)
 
     def table(target, values, slots_at):
-        total = jnp.zeros((tokens, slots_at.shape[1]), jnp.int32)
-        for k in range(target.shape[1]):
-            total = total + jnp.where(target[:, k:k + 1] == slots_at, values[:, k:k + 1], 0)
+        total = jnp.zeros((slots_at.shape[0], tokens), jnp.int32)
+        for k in range(target.shape[0]):
+            total = total + jnp.where(target[k:k + 1] == slots_at, values[k:k + 1], 0)
         return total
 
-    lanes = ((experts * group + 127) // 128) * 128
-    place = lax.broadcasted_iota(jnp.int32, (tokens, lanes), 1)
+    used = experts * group
+    place = lax.broadcasted_iota(jnp.int32, (used, tokens), 0)
     inside = lax.rem(place, group)
     owner = lax.div(place, group)
     slots_x = jnp.where(inside < capacity, owner * capacity + inside, -2)
     slots_c = jnp.where(inside >= capacity, owner * capacity + inside - capacity, -2)
     ones = jnp.ones(target_f.shape, jnp.int32)
-    used = experts * group
-    pick_x = table(target_f, ones, slots_x).astype(F32).T[:used].astype(BF16)
-    pick_c = table(target_b, ones, slots_c).astype(F32).T[:used].astype(BF16)
+    pick_x = table(target_f, ones, slots_x).astype(F32).astype(BF16)
+    pick_c = table(target_b, ones, slots_c).astype(F32).astype(BF16)
     scale_c = jnp.sum(
-        table(target_b, level[1], slots_c).astype(F32).T[:used], axis=1, keepdims=True
+        table(target_b, level[1], slots_c).astype(F32), axis=1, keepdims=True
     ) / 4096.0
 
     parts = ne * nt * group
-    lanes = ((parts + 127) // 128) * 128
-    place = lax.broadcasted_iota(jnp.int32, (tokens, lanes), 1)
+    place = lax.broadcasted_iota(jnp.int32, (parts, tokens), 0)
     inside = lax.rem(place, group)
     owner = lax.div(place, 2 * nt * group)
     slots_o = jnp.where(inside < capacity, owner * capacity + inside, -2)
@@ -148,9 +146,9 @@
     level_o = table(target_f, level[0], slots_o)
     high = lax.div(level_o, 64)
     low = level_o - high * 64
-    factor_high = (high.astype(F32) / 64.0).astype(BF16)[:, :parts]
-    factor_low = (low.astype(F32) / 4096.0).astype(BF16)[:, :parts]
-    factor_grad = table(target_b, ones, slots_g).astype(F32).astype(BF16)[:, :parts]
+    factor_high = (high.astype(F32) / 64.0).T.astype(BF16)
+    factor_low = (low.astype(F32) / 4096.0).T.astype(BF16)
+    factor_grad = table(target_b, ones, slots_g).astype(F32).T.astype(BF16)
 
     saved_local.wait()
     for copy in saved_copies:
@@ -275,26 +273,26 @@
     ).astype(BF16)
     up_grad_r = jnp.where(ahead, 0.0, grad_hidden * swish(gate_back)).astype(BF16)
     cw = chunk_of(width)
-    for c in range(nt):
-        def routed_second(n, carry, c=c):
+    ret_copies = []
+    for st in list(range(1, nt)) + [0]:
+        to_t = peer_t(st)
+
+        def routed_second(n, carry, to_t=to_t):
             at = pl.ds(pl.multiple_of(n * cw, 128), cw)
-            cols = pl.ds(pl.multiple_of(c * width + n * cw, 128), cw)
+            cols = pl.ds(pl.multiple_of(to_t * width + n * cw, 128), cw)
             total = (
                 dot(hidden_r, down_r[:, cols])
                 + contract_last(gate_grad_r, gate_r[cols, :])
                 + contract_last(up_grad_r, up_r[cols, :])
             )
             for i in range(ne):
-                ret_send[i, c, :, at] = total[i * group:(i + 1) * group].astype(BF16)
+                ret_send[i, to_t, :, at] = total[i * group:(i + 1) * group].astype(BF16)
             return carry
 
         lax.fori_loop(0, width // cw, routed_second, 0)
-
-    ret_copies = []
-    for se in range(ne):
-        for st in range(nt):
+        for se in range(ne):
             if se or st:
-                to_e, to_t = peer_e(se), peer_t(st)
+                to_e = peer_e(se)
                 n = se * nt + st - 1
                 copy = remote(
                     ret_send.at[to_e, to_t], ret_recv.at[me_e, me_t],
@@ -359,6 +357,10 @@
         + part_copies
     ):
         copy.wait_send()
+
+
+def lanes_last(choices):
+    return jnp.swapaxes(choices[:, 0], 1, 2)
 
 
 def local(
@@ -433,7 +435,7 @@
         name="moe_step",
     )(
         inputs_prev[0], cotangent_next[0], saved_input[0],
-        expert_ids[:, 0], keep_mask[:, 0], slot_pos[:, 0], weight_q[:, 0],
+        *(lanes_last(v) for v in (expert_ids, keep_mask, slot_pos, weight_q)),
         gate_routed[0, 0], up_routed[0, 0], down_routed[0, 0],
         gate_shared[0], up_shared[0], down_shared[0],
     )

time: 58.1 us -> 51.7 us (0.89)
  local copies, waits for them, and re-layouts: 9.57 us -> 3.63 us
    unnamed x6 -> x2, local copies, waits for them, and re-layouts: 9.57 us -> 3.63 us
where the time goes in v3:
time: 51.7 us; the launch traced here: 51.4 us
  Pallas kernels  47.2 us (91%)
  local copies, waits for them, and re-layouts  3.63 us (7%)
  between operations  0.64 us (1%)
    pallas_call x1, Pallas kernels, local(): pl.pallas_call(functools.partial(kernel, (n_pipe, ne, nt, capacity)), out...  47.2 us
    unnamed x2, local copies, waits for them, and re-layouts  3.63 us

profile of v3, /device:TPU:0, one launch (start us, length us, event | category | flops | bytes accessed | tf_op | source)
XLA Modules:
  0.0 51.4 jit_solution(8823779077847717748)
XLA Ops:
  0.6 47.2 %moe_step.1 = (bf16[128,1792]{1,0:T(8,128)(2,1)}, bf16[128,1792]{1,0:T(8,128)(2,1)}) custom-call(bf16[128,1792]{1,0:T(8,128)(2,1)} %bitcast.31, bf16[128,1792]{1,0:T(8,128)(2,1)} %bitcast.32, bf16[128,1792]{1,0:T(8,128)(2,1)} %bitcast.33, s32[2,8,128]{2,1,0:T(8,128)} %bitcast.34, s32[2,8,128]{2,1,0:T(8,128)} %bitcast.35, s32[2,8,128]{2,1,0:T(8,128)} %bitcast.36, ...), custom_call_target="tpu_custom_call" | custom-call | tf_op jit(solution)/shard_map/moe_step/pallas_call | solution.py:381
  47.8 1.8 %copy.17 = bf16[1,128,1792]{2,1,0:T(8,128)(2,1)} copy(bf16[1,128,1792]{2,1,0:T(8,128)(2,1)} %bitcast.30) | data formatting | bytes 917504
  49.6 1.8 %copy.18 = bf16[1,128,1792]{2,1,0:T(8,128)(2,1)} copy(bf16[1,128,1792]{2,1,0:T(8,128)(2,1)} %bitcast.29) | data formatting | bytes 917504
